TPU v7x, 32 devices: a whole 2x2x4 slice. The times are simulated.
32 devices in a mesh: dp: 2 (over x), ei: 4 (over z), eo: 4 (over y, core).
Axes of the slice: x: 2, y: 2, z: 4, core: 2. Of those that a mesh axis runs over, the one named last changes fastest.
Arguments:
- x_in: bfloat16 [8192, 1024], P(('dp', 'ei', 'eo')), parts along dimension 0
- expert_idx: int32 [8192, 8], P(('dp', 'ei', 'eo')), parts along dimension 0
- gate_val: float32 [8192, 8], P(('dp', 'ei', 'eo')), parts along dimension 0
- w_gate: bfloat16 [32, 1024, 512], P(('ei', 'eo'))
- w_up: bfloat16 [32, 1024, 512], P(('ei', 'eo'))
- w_down: bfloat16 [32, 512, 1024], P(('ei', 'eo'))
- dy_in: bfloat16 [8192, 1024], P(('dp', 'ei', 'eo')), parts along dimension 0
Outputs:
- output 1: bfloat16 [8192, 1024], P(('dp', 'ei', 'eo')), parts along dimension 0
- output 2: bfloat16 [8192, 1024], P(('dp', 'ei', 'eo')), parts along dimension 0
- output 3: float32 [8192, 8], P(('dp', 'ei', 'eo')), parts along dimension 0
- output 4: float32 [64, 1024, 512], P(('dp', 'ei', 'eo')), parts along dimension 0
- output 5: float32 [64, 1024, 512], P(('dp', 'ei', 'eo')), parts along dimension 0
- output 6: float32 [64, 512, 1024], P(('dp', 'ei', 'eo')), parts along dimension 0
There are 2 independent parts. A program takes and returns all parts, laid end to end along the dimension named above; an argument that names none is the same for every part.
All inputs are finite; a program needn't handle non-finite values.
Results may differ from a plain program's by a relative error of at most 0.00783561.
Values are sent between devices in bfloat16 or wider.
A program may use at most 1 GiB of HBM per device.

v0:
```python
import jax
import jax.numpy as jnp
from jax import lax
from jax.sharding import PartitionSpec as P

SKEW_FACTOR = 4


def route_slots(dev_idx, experts, group_devs, capacity):
    tok_count, top_k = dev_idx.shape
    n_assign = tok_count * top_k
    flat_exp = dev_idx.reshape(n_assign)
    sort_order = jnp.argsort(flat_exp, stable=True).astype(jnp.int32)
    sorted_exp = flat_exp[sort_order]
    counts = jax.ops.segment_sum(jnp.ones((n_assign,), jnp.int32), flat_exp, num_segments=experts)
    starts = jnp.cumsum(counts) - counts
    within = jnp.arange(n_assign, dtype=jnp.int32) - starts[sorted_exp]
    exp_local = experts // group_devs
    slot_sorted = (((sorted_exp % exp_local) * group_devs + sorted_exp // exp_local) * capacity + within).astype(jnp.int32)
    slot_of = jnp.zeros((n_assign,), jnp.int32).at[sort_order].set(slot_sorted)
    slot_owner = jnp.full((experts * capacity,), -1, jnp.int32).at[slot_sorted].set(sort_order)
    return slot_of, slot_owner


def expert_forward(x_rows, wg_loc, wu_loc, wd_loc):
    pre_gate = jnp.einsum('ecd,edf->ecf', x_rows, wg_loc, preferred_element_type=jnp.float32)
    pre_up = jnp.einsum('ecd,edf->ecf', x_rows, wu_loc, preferred_element_type=jnp.float32)
    sig_gate = jax.nn.sigmoid(pre_gate)
    hidden = (pre_gate * sig_gate * pre_up).astype(jnp.bfloat16)
    out_rows = jnp.einsum('ecf,efd->ecd', hidden, wd_loc, preferred_element_type=jnp.float32).astype(jnp.bfloat16)
    return out_rows, (pre_gate, pre_up, sig_gate, hidden)


def expert_backward(x_rows, do_rows, saved_acts, wg_loc, wu_loc, wd_loc):
    pre_gate, pre_up, sig_gate, hidden = saved_acts
    silu_gate = pre_gate * sig_gate
    dw_down = jnp.einsum('ecf,ecd->efd', hidden, do_rows, preferred_element_type=jnp.float32)
    d_hidden = jnp.einsum('ecd,efd->ecf', do_rows, wd_loc, preferred_element_type=jnp.float32)
    d_gate = (d_hidden * pre_up * sig_gate * (1.0 + pre_gate * (1.0 - sig_gate))).astype(jnp.bfloat16)
    d_up = (d_hidden * silu_gate).astype(jnp.bfloat16)
    dw_gate = jnp.einsum('ecd,ecf->edf', x_rows, d_gate, preferred_element_type=jnp.float32)
    dw_up = jnp.einsum('ecd,ecf->edf', x_rows, d_up, preferred_element_type=jnp.float32)
    dx_rows = (jnp.einsum('ecf,edf->ecd', d_gate, wg_loc, preferred_element_type=jnp.float32) + jnp.einsum('ecf,edf->ecd', d_up, wu_loc, preferred_element_type=jnp.float32)).astype(jnp.bfloat16)
    return dx_rows, dw_gate, dw_up, dw_down


def to_experts(row_data, exp_local, ei_size, eo_size, capacity):
    row_width = row_data.shape[-1]
    buffer = row_data.reshape(exp_local, ei_size, eo_size, capacity, row_width)
    buffer = lax.all_to_all(buffer, 'eo', 2, 2, tiled=True)
    buffer = lax.all_to_all(buffer, 'ei', 1, 1, tiled=True)
    return buffer.reshape(exp_local, ei_size * eo_size * capacity, row_width)


def to_tokens(row_data, ei_size, eo_size, capacity):
    exp_local, n_rows, row_width = row_data.shape
    buffer = row_data.reshape(exp_local, ei_size, eo_size, capacity, row_width)
    buffer = lax.all_to_all(buffer, 'ei', 1, 1, tiled=True)
    buffer = lax.all_to_all(buffer, 'eo', 2, 2, tiled=True)
    return buffer.reshape(exp_local * n_rows, row_width)


def solution(mesh):
    ei_size = mesh.shape['ei']
    eo_size = mesh.shape['eo']
    group_devs = ei_size * eo_size
    tok_spec = P(('dp', 'ei', 'eo'), None)
    weight_spec = P(('ei', 'eo'), None, None)
    grad_spec = P(('dp', 'ei', 'eo'), None, None)

    def device_layer(x_loc, idx_loc, gate_loc, wg_loc, wu_loc, wd_loc, dy_loc):
        tok_count, top_k = idx_loc.shape
        d_model = x_loc.shape[1]
        exp_local = wg_loc.shape[0]
        experts = exp_local * group_devs
        capacity = SKEW_FACTOR * ((tok_count * top_k + experts - 1) // experts)
        slot_of, slot_owner = route_slots(idx_loc, experts, group_devs, capacity)
        has_row = slot_owner >= 0
        safe_owner = jnp.where(has_row, slot_owner, 0)
        tok_of_slot = safe_owner // top_k
        x_recv = to_experts(x_loc[tok_of_slot], exp_local, ei_size, eo_size, capacity)
        out_rows, saved_acts = expert_forward(x_recv, wg_loc, wu_loc, wd_loc)
        out_back = to_tokens(out_rows, ei_size, eo_size, capacity)
        out_tok = out_back[slot_of].reshape(tok_count, top_k, d_model)
        y_loc = jnp.sum(gate_loc[:, :, None] * out_tok, axis=1).astype(jnp.bfloat16)
        dgate_loc = jnp.einsum('td,tkd->tk', dy_loc, out_tok, preferred_element_type=jnp.float32)
        slot_gate = jnp.where(has_row, gate_loc.reshape(tok_count * top_k)[safe_owner], 0.0)
        do_send = (slot_gate[:, None] * dy_loc[tok_of_slot]).astype(jnp.bfloat16)
        do_recv = to_experts(do_send, exp_local, ei_size, eo_size, capacity)
        dx_rows, dw_gate, dw_up, dw_down = expert_backward(x_recv, do_recv, saved_acts, wg_loc, wu_loc, wd_loc)
        dx_back = to_tokens(dx_rows, ei_size, eo_size, capacity)
        dx_loc = jnp.sum(dx_back[slot_of].reshape(tok_count, top_k, d_model).astype(jnp.float32), axis=1).astype(jnp.bfloat16)
        return y_loc, dx_loc, dgate_loc, dw_gate, dw_up, dw_down

    return jax.shard_map(device_layer, mesh=mesh, in_specs=(tok_spec, tok_spec, tok_spec, weight_spec, weight_spec, weight_spec, tok_spec), out_specs=(tok_spec, tok_spec, tok_spec, grad_spec, grad_spec, grad_spec), check_vma=False)
```

profile of v0, /device:TPU:0, one launch (start us, length us, event | category | flops | bytes accessed | tf_op | source)
XLA Modules:
  0.0 2466.3 jit_solution(5959131509483649363)
XLA Ops:
  1.8 14.7 scatter_custom_fusion
  40.6 16.4 fusion.14
  65.2 35.4 %gather_fusion.1 = bf16[8192,1024]{1,0:T(8,128)(2,1)} fusion(bf16[256,1024]{1,0:T(8,128)(2,1)S(1)} %copy-done.2, s32[8192]{0:T(1024)S(1)} %get-tuple-element.41), kind=kCustom, calls=%fused_computation.1 | custom fusion | bytes 33587200 | tf_op jit(solution)/shard_map/gather | solution.py:81
  100.6 13.9 copy.47
  122.4 45.5 %gather_fusion.3 = f32[8192]{0:T(1024)S(1)} fusion(f32[2048]{0:T(1024)S(1)} %reshape.200, s32[8192]{0:T(1024)S(1)} %get-tuple-element.40), kind=kCustom, calls=%fused_computation.3 | custom fusion | bytes 98304 | tf_op jit(solution)/shard_map/gather | solution.py:87
  168.0 35.4 %gather_fusion.4 = bf16[8192,1024]{1,0:T(8,128)(2,1)} fusion(bf16[256,1024]{1,0:T(8,128)(2,1)S(1)} %copy-done.3, s32[8192]{0:T(1024)S(1)} %get-tuple-element.41), kind=kCustom, calls=%fused_computation.4 | custom fusion | bytes 33587200 | tf_op jit(solution)/shard_map/gather | solution.py:88
  203.4 14.6 fusion
  218.0 87.0 %all-to-all-done = bf16[2,4,4,256,1024]{4,3,1,0,2:T(8,128)(2,1)} async-done(((bf16[2,4,4,256,1024]{4,3,1,0,2:T(8,128)(2,1)}), bf16[2,4,4,256,1024]{4,3,1,0,2:T(8,128)(2,1)}, u32[]{:S(2)}, u32[]{:S(2)}) %all-to-all-start) | async-done | bytes 16777248 | tf_op jit(solution)/shard_map/all_to_all | solution.py:50
  312.0 13.9 copy.48
  325.9 168.8 %all-to-all-done.4 = bf16[2,4,4,256,1024]{4,3,1,0,2:T(8,128)(2,1)} async-done(((bf16[2,4,4,256,1024]{4,3,1,0,2:T(8,128)(2,1)}), bf16[2,4,4,256,1024]{4,3,1,0,2:T(8,128)(2,1)}, u32[]{:S(2)}, u32[]{:S(2)}) %all-to-all-start.4) | async-done | bytes 16777248 | tf_op jit(solution)/shard_map/all_to_all | solution.py:50
  501.7 13.9 copy.56
  515.6 349.4 %all-to-all-done.1 = bf16[2,4,4,256,1024]{4,3,2,0,1:T(8,128)(2,1)} async-done(((bf16[2,4,4,256,1024]{4,3,2,0,1:T(8,128)(2,1)}), bf16[2,4,4,256,1024]{4,3,2,0,1:T(8,128)(2,1)}, u32[]{:S(2)}, u32[]{:S(2)}) %all-to-all-start.1) | async-done | bytes 16777248 | tf_op jit(solution)/shard_map/all_to_all | solution.py:51
  886.1 18.5 fusion.29
  904.6 18.5 fusion.28
  923.1 311.1 %all-to-all-done.5 = bf16[2,4,4,256,1024]{4,3,2,0,1:T(8,128)(2,1)} async-done(((bf16[2,4,4,256,1024]{4,3,2,0,1:T(8,128)(2,1)}), bf16[2,4,4,256,1024]{4,3,2,0,1:T(8,128)(2,1)}, u32[]{:S(2)}, u32[]{:S(2)}) %all-to-all-start.5) | async-done | bytes 16777248 | tf_op jit(solution)/shard_map/all_to_all | solution.py:51
  1248.1 31.0 %multiply_convert_fusion = (bf16[2,4096,512]{2,1,0:T(8,128)(2,1)}, bf16[2,4096,512]{2,1,0:T(8,128)(2,1)}, bf16[2,4096,512]{2,1,0:T(8,128)(2,1)}) fusion(f32[2,4096,512]{2,1,0:T(8,128)} %fusion.28, f32[2,4096,512]{2,1,0:T(8,128)} %fusion.29, bf16[2,4096,1024]{2,1,0:T(8,128)(2,1)} %bitcast.83, bf16[2,512,1024]{2,1,0:T(8,128)(2,1)S(1)} %copy-done), kind=kOutput, calls=%fused_computation.12 | convolution fusion | flops 8652849152 | bytes 77594624 | tf_op jit(solution)/shard_map/ecd,efd->ecf/dot_general | solution.py:38
  1279.1 15.8 convolution_convert_fusion
  1294.9 13.9 copy.50
  1316.1 18.7 fusion.30
  1334.9 23.5 add_convert_fusion
  1372.3 305.9 %all-to-all-done.2 = bf16[2,4,4,256,1024]{4,3,2,0,1:T(8,128)(2,1)} async-done(((bf16[2,4,4,256,1024]{4,3,2,0,1:T(8,128)(2,1)}), bf16[2,4,4,256,1024]{4,3,2,0,1:T(8,128)(2,1)}, u32[]{:S(2)}, u32[]{:S(2)}) %all-to-all-start.2) | async-done | bytes 16777248 | tf_op jit(solution)/shard_map/all_to_all | solution.py:58
  1685.2 13.9 copy.51
  1699.1 348.2 %all-to-all-done.6 = bf16[2,4,4,256,1024]{4,3,2,0,1:T(8,128)(2,1)} async-done(((bf16[2,4,4,256,1024]{4,3,2,0,1:T(8,128)(2,1)}), bf16[2,4,4,256,1024]{4,3,2,0,1:T(8,128)(2,1)}, u32[]{:S(2)}, u32[]{:S(2)}) %all-to-all-start.6) | async-done | bytes 16777248 | tf_op jit(solution)/shard_map/all_to_all | solution.py:58
  2054.3 13.9 copy.59
  2068.2 168.8 %all-to-all-done.3 = bf16[2,4,4,256,1024]{4,3,1,0,2:T(8,128)(2,1)} async-done(((bf16[2,4,4,256,1024]{4,3,1,0,2:T(8,128)(2,1)}), bf16[2,4,4,256,1024]{4,3,1,0,2:T(8,128)(2,1)}, u32[]{:S(2)}, u32[]{:S(2)}) %all-to-all-start.3) | async-done | bytes 16777248 | tf_op jit(solution)/shard_map/all_to_all | solution.py:59
  2252.2 16.4 fusion.32
  2268.5 16.2 fusion.31
  2284.7 16.6 fusion.33
  2315.1 18.9 gather_fusion.2
  2345.2 81.4 %all-to-all-done.7 = bf16[2,4,4,256,1024]{4,3,1,0,2:T(8,128)(2,1)} async-done(((bf16[2,4,4,256,1024]{4,3,1,0,2:T(8,128)(2,1)}), bf16[2,4,4,256,1024]{4,3,1,0,2:T(8,128)(2,1)}, u32[]{:S(2)}, u32[]{:S(2)}) %all-to-all-start.7) | async-done | bytes 16777248 | tf_op jit(solution)/shard_map/all_to_all | solution.py:59
  2426.6 14.0 copy.60
  2440.7 19.1 gather_fusion.5
  (59 shorter events, 171.8 us)
Async XLA Ops:
  0.6 1247.5 %copy-start = (bf16[2,512,1024]{2,1,0:T(8,128)(2,1)S(1)}, bf16[2,512,1024]{2,1,0:T(8,128)(2,1)}, u32[]{:S(2)}) copy-start(bf16[2,512,1024]{2,1,0:T(8,128)(2,1)} %param.12) | copy-start | bytes 6291460
  0.6 64.5 %copy-start.2 = (bf16[256,1024]{1,0:T(8,128)(2,1)S(1)}, bf16[256,1024]{1,0:T(8,128)(2,1)}, u32[]{:S(2)}) copy-start(bf16[256,1024]{1,0:T(8,128)(2,1)} %param.7) | copy-start | bytes 1572868
  114.5 7.1 copy-start.7
  114.5 190.6 %all-to-all-start = ((bf16[2,4,4,256,1024]{4,3,1,0,2:T(8,128)(2,1)}), bf16[2,4,4,256,1024]{4,3,1,0,2:T(8,128)(2,1)}, u32[]{:S(2)}, u32[]{:S(2)}) async-start(bf16[2,4,4,256,1024]{4,3,1,0,2:T(8,128)(2,1)} %copy.47), calls=%async_computation | async-start | bytes 33554432 | tf_op jit(solution)/shard_map/all_to_all | solution.py:50
  121.7 0.7 copy-start.5
  122.4 45.6 %copy-start.3 = (bf16[256,1024]{1,0:T(8,128)(2,1)S(1)}, bf16[256,1024]{1,0:T(8,128)(2,1)}, u32[]{:S(2)}) copy-start(bf16[256,1024]{1,0:T(8,128)(2,1)} %param.13) | copy-start | bytes 1572868
  305.1 189.7 %all-to-all-start.4 = ((bf16[2,4,4,256,1024]{4,3,1,0,2:T(8,128)(2,1)}), bf16[2,4,4,256,1024]{4,3,1,0,2:T(8,128)(2,1)}, u32[]{:S(2)}, u32[]{:S(2)}) async-start(bf16[2,4,4,256,1024]{4,3,1,0,2:T(8,128)(2,1)} %fusion), calls=%async_computation.4 | async-start | bytes 33554432 | tf_op jit(solution)/shard_map/all_to_all | solution.py:50
  494.7 370.2 %all-to-all-start.1 = ((bf16[2,4,4,256,1024]{4,3,2,0,1:T(8,128)(2,1)}), bf16[2,4,4,256,1024]{4,3,2,0,1:T(8,128)(2,1)}, u32[]{:S(2)}, u32[]{:S(2)}) async-start(bf16[2,4,4,256,1024]{4,3,2,0,1:T(8,128)(2,1)} %copy.48), calls=%async_computation.1 | async-start | bytes 33554432 | tf_op jit(solution)/shard_map/all_to_all | solution.py:51
  865.0 369.3 %all-to-all-start.5 = ((bf16[2,4,4,256,1024]{4,3,2,0,1:T(8,128)(2,1)}), bf16[2,4,4,256,1024]{4,3,2,0,1:T(8,128)(2,1)}, u32[]{:S(2)}, u32[]{:S(2)}) async-start(bf16[2,4,4,256,1024]{4,3,2,0,1:T(8,128)(2,1)} %copy.56), calls=%async_computation.5 | async-start | bytes 33554432 | tf_op jit(solution)/shard_map/all_to_all | solution.py:51
  1308.8 7.3 copy-start.8
  1308.8 369.4 %all-to-all-start.2 = ((bf16[2,4,4,256,1024]{4,3,2,0,1:T(8,128)(2,1)}), bf16[2,4,4,256,1024]{4,3,2,0,1:T(8,128)(2,1)}, u32[]{:S(2)}, u32[]{:S(2)}) async-start(bf16[2,4,4,256,1024]{4,3,2,0,1:T(8,128)(2,1)} %copy.50), calls=%async_computation.2 | async-start | bytes 33554432 | tf_op jit(solution)/shard_map/all_to_all | solution.py:58
  1678.2 369.0 %all-to-all-start.6 = ((bf16[2,4,4,256,1024]{4,3,2,0,1:T(8,128)(2,1)}), bf16[2,4,4,256,1024]{4,3,2,0,1:T(8,128)(2,1)}, u32[]{:S(2)}, u32[]{:S(2)}) async-start(bf16[2,4,4,256,1024]{4,3,2,0,1:T(8,128)(2,1)} %copy.58), calls=%async_computation.6 | async-start | bytes 33554432 | tf_op jit(solution)/shard_map/all_to_all | solution.py:58
  2047.3 189.7 %all-to-all-start.3 = ((bf16[2,4,4,256,1024]{4,3,1,0,2:T(8,128)(2,1)}), bf16[2,4,4,256,1024]{4,3,1,0,2:T(8,128)(2,1)}, u32[]{:S(2)}, u32[]{:S(2)}) async-start(bf16[2,4,4,256,1024]{4,3,1,0,2:T(8,128)(2,1)} %copy.51), calls=%async_computation.3 | async-start | bytes 33554432 | tf_op jit(solution)/shard_map/all_to_all | solution.py:59
  2237.0 189.7 %all-to-all-start.7 = ((bf16[2,4,4,256,1024]{4,3,1,0,2:T(8,128)(2,1)}), bf16[2,4,4,256,1024]{4,3,1,0,2:T(8,128)(2,1)}, u32[]{:S(2)}, u32[]{:S(2)}) async-start(bf16[2,4,4,256,1024]{4,3,1,0,2:T(8,128)(2,1)} %copy.59), calls=%async_computation.7 | async-start | bytes 33554432 | tf_op jit(solution)/shard_map/all_to_all | solution.py:59
  2315.1 18.9 copy-start.4
  2315.1 24.5 copy-start.6
  2440.7 25.4 %copy-start.1 = (bf16[2,512,1024]{2,1,0:T(8,128)(2,1)S(1)}, bf16[2,512,1024]{2,1,0:T(8,128)(2,1)}, u32[]{:S(2)}) copy-start(bf16[2,512,1024]{2,1,0:T(8,128)(2,1)} %param.12) | copy-start | bytes 6291460
where the time goes:
time: 2470 us
  waiting for transfers between devices  1820 us (74%)
  local copies, waits for them, and re-layouts  339 us (14%)
  matrix products  180 us (7%)
  other arithmetic  68.5 us (3%)
  starting transfers between devices  56.5 us (2%)
    all_to_all x2, waiting for transfers between devices, to_experts(): buffer = lax.all_to_all(buffer, 'ei', 1, 1, tiled=True)  661 us
    all_to_all x2, waiting for transfers between devices, to_tokens(): buffer = lax.all_to_all(buffer, 'ei', 1, 1, tiled=True)  654 us
    all_to_all x2, waiting for transfers between devices, to_experts(): buffer = lax.all_to_all(buffer, 'eo', 2, 2, tiled=True)  256 us
    all_to_all x2, waiting for transfers between devices, to_tokens(): buffer = lax.all_to_all(buffer, 'eo', 2, 2, tiled=True)  250 us
  transfers between devices with their start and end apart: 8, of which 8 were waited for; matrix products, arithmetic and copies ran while one was open for 15% of the time, Pallas kernels for 0%

commit v1 on v0

v1 whole, which is shorter than its diff:
```python
import jax
import jax.numpy as jnp
from jax import lax
from jax.sharding import PartitionSpec as P

GROUP = ('ei', 'eo')


def solution(mesh):
    group_devs = mesh.shape['ei'] * mesh.shape['eo']
    eo_size = mesh.shape['eo']
    tok_spec = P(('dp', 'ei', 'eo'), None)
    weight_spec = P(('ei', 'eo'), None, None)
    grad_spec = P(('dp', 'ei', 'eo'), None, None)

    def device_layer(x_loc, idx_loc, gate_loc, wg_loc, wu_loc, wd_loc, dy_loc):
        tok_count, top_k = idx_loc.shape
        d_model = x_loc.shape[1]
        exp_local = wg_loc.shape[0]
        experts = exp_local * group_devs
        me = lax.axis_index('ei') * eo_size + lax.axis_index('eo')
        dense_gate = jnp.sum(jnp.where(idx_loc[:, :, None] == jnp.arange(experts), gate_loc[:, :, None], 0.0), axis=1)
        gate_all = lax.all_to_all(dense_gate.reshape(tok_count, group_devs, exp_local).transpose(1, 0, 2), GROUP, 0, 0, tiled=True)
        gate_all = gate_all.reshape(group_devs * tok_count, exp_local)
        x_all = lax.all_gather(x_loc, GROUP, axis=0, tiled=True)
        dy_all = lax.all_gather(dy_loc, GROUP, axis=0, tiled=True)
        y_part = jnp.zeros((group_devs * tok_count, d_model), jnp.float32)
        dx_part = jnp.zeros((group_devs * tok_count, d_model), jnp.float32)
        saved = []
        dgates = []
        for e in range(exp_local):
            gate_e = gate_all[:, e:e + 1]
            routed = gate_e > 0.0
            x_e = jnp.where(routed, x_all, 0)
            a = jnp.dot(x_e, wg_loc[e], preferred_element_type=jnp.float32)
            b = jnp.dot(x_e, wu_loc[e], preferred_element_type=jnp.float32)
            s = jax.nn.sigmoid(a)
            h = (a * s * b).astype(jnp.bfloat16)
            o = jnp.dot(h, wd_loc[e], preferred_element_type=jnp.float32).astype(jnp.bfloat16).astype(jnp.float32)
            y_part = y_part + gate_e * o
            dgates.append(jnp.sum(dy_all.astype(jnp.float32) * o, axis=1))
            saved.append((x_e, a, b, s, h, gate_e))
        y_loc = lax.psum_scatter(y_part, GROUP, scatter_dimension=0, tiled=True).astype(jnp.bfloat16)
        grads = []
        for e in range(exp_local):
            x_e, a, b, s, h, gate_e = saved[e]
            g = jnp.where(gate_e > 0.0, (gate_e * dy_all).astype(jnp.bfloat16), 0)
            dh = lax.dot_general(g, wd_loc[e], (((1,), (1,)), ((), ())), preferred_element_type=jnp.float32)
            da = (dh * b * s * (1.0 + a * (1.0 - s))).astype(jnp.bfloat16)
            db = (dh * (a * s)).astype(jnp.bfloat16)
            dx = (lax.dot_general(da, wg_loc[e], (((1,), (1,)), ((), ())), preferred_element_type=jnp.float32)
                  + lax.dot_general(db, wu_loc[e], (((1,), (1,)), ((), ())), preferred_element_type=jnp.float32)).astype(jnp.bfloat16)
            dx_part = dx_part + dx.astype(jnp.float32)
            grads.append((x_e, da, db, h, g))
        dx_loc = lax.psum_scatter(dx_part, GROUP, scatter_dimension=0, tiled=True).astype(jnp.bfloat16)

        def tdot(p, q):
            return lax.dot_general(p, q, (((0,), (0,)), ((), ())), preferred_element_type=jnp.float32)

        dw_gate = jnp.stack([tdot(x_e, da) for x_e, da, db, h, g in grads])
        dw_up = jnp.stack([tdot(x_e, db) for x_e, da, db, h, g in grads])
        dw_down = jnp.stack([tdot(h, g) for x_e, da, db, h, g in grads])
        dg = jnp.stack(dgates, axis=1).reshape(group_devs, tok_count, exp_local)
        dg = lax.all_to_all(dg, GROUP, 0, 0, tiled=True).transpose(1, 0, 2).reshape(tok_count, experts)
        dgate_loc = jnp.sum(jnp.where(idx_loc[:, :, None] == jnp.arange(experts), dg[:, None, :], 0.0), axis=2)
        return y_loc, dx_loc, dgate_loc, dw_gate, dw_up, dw_down

    return jax.shard_map(device_layer, mesh=mesh, in_specs=(tok_spec, tok_spec, tok_spec, weight_spec, weight_spec, weight_spec, tok_spec), out_specs=(tok_spec, tok_spec, tok_spec, grad_spec, grad_spec, grad_spec), check_vma=False)
```

time: 2470 us -> 633 us (0.26)
  waiting for transfers between devices: 1820 us -> 374 us
  local copies, waits for them, and re-layouts: 339 us -> 5.91 us
  other arithmetic: 68.5 us -> 11.8 us
  starting transfers between devices: 56.5 us -> 3.87 us
    all_to_all x8 -> x1, waiting for transfers between devices: 1820 us -> 0.01 us  [device_layer(): lax.all_to_all(dg, GROUP, 0, 0, tiled=True).transpose(1, 0, 2)]
    reduce_scatter x0 -> x2, waiting for transfers between devices: none -> 248 us  [the longest x1 177 us: device_layer(): lax.psum_scatter(dx_part, GROUP, scatter_dimension=0, tiled=True)]
    gather x8 -> x0, local copies, waits for them, and re-layouts: 168 us -> none  [the longest x1 45.5 us: device_layer(): gate_loc.reshape(tok_count * top_k)[safe_owner]]
    all_gather x0 -> x2, waiting for transfers between devices: none -> 126 us  [the longest x1 64.9 us: device_layer(): x_all = lax.all_gather(x_loc, GROUP, axis=0, tiled=True)]
    all_to_all x8 -> x0, local copies, waits for them, and re-layouts: 111 us -> none  [the longest x2 27.9 us: to_tokens(): buffer = lax.all_to_all(buffer, 'eo', 2, 2, tiled=True)]
    all_to_all x8 -> x1, starting transfers between devices: 56.5 us -> 3.71 us  [device_layer(): lax.all_to_all(dg, GROUP, 0, 0, tiled=True).transpose(1, 0, 2)]
    reshape x5 -> x1, local copies, waits for them, and re-layouts: 41.8 us -> 0.02 us  [device_layer(): dense_gate.reshape(tok_count, group_devs, exp_local).transpose(1, 0, 2)]
    dot_general x10 -> x18, matrix products: 180 us -> 200 us  [the longest x6 38 us: tdot(): lax.dot_general(p, q, (((0,), (0,)), ((), ())), preferred_element_type=jn...]
  transfers between devices with their start and end apart: 8 -> 5, of which waited for: 8 -> 4; matrix products, arithmetic and copies ran while one was open for 15% -> 20% of each run, Pallas kernels for 0% -> 0%
where the time goes in v1:
time: 633 us; the launch traced here: 624 us
  waiting for transfers between devices  374 us (59%)
  matrix products  200 us (32%)
  between operations  14.5 us (2%)
  blocking collectives  13.9 us (2%)
  other arithmetic  11.8 us (2%)
    reduce_scatter x1, waiting for transfers between devices, device_layer(): lax.psum_scatter(dx_part, GROUP, scatter_dimension=0, tiled=True)  177 us
    reduce_scatter x1, waiting for transfers between devices, device_layer(): lax.psum_scatter(y_part, GROUP, scatter_dimension=0, tiled=True)  71.6 us
    all_gather x1, waiting for transfers between devices, device_layer(): x_all = lax.all_gather(x_loc, GROUP, axis=0, tiled=True)  64.9 us
    all_gather x1, waiting for transfers between devices, device_layer(): dy_all = lax.all_gather(dy_loc, GROUP, axis=0, tiled=True)  60.8 us
    dot_general x6, matrix products, tdot(): lax.dot_general(p, q, (((0,), (0,)), ((), ())), preferred_element_type=jn...  38 us
    dot_general x2, matrix products, device_layer(): lax.dot_general(g, wd_loc[e], (((1,), (1,)), ((), ())), preferred_element...  36.2 us
    dot_general x2, matrix products, device_layer(): jnp.dot(h, wd_loc[e], preferred_element_type=jnp.float32)  35.9 us
    dot_general x2, matrix products, device_layer(): lax.dot_general(db, wu_loc[e], (((1,), (1,)), ((), ())), preferred_elemen...  32.3 us
  transfers between devices with their start and end apart: 5, of which 4 were waited for; matrix products, arithmetic and copies ran while one was open for 20% of the time, Pallas kernels for 0%

profile of v1, /device:TPU:0, one launch (start us, length us, event | category | flops | bytes accessed | tf_op | source)
XLA Modules:
  0.0 623.8 jit_solution(10502864751805902640)
XLA Ops:
  7.2 2.0 copy.32
  9.3 2.0 copy.33
  11.4 0.8 select_reduce_fusion.1
  12.2 13.9 %all_to_all.10 = f32[16,256,2]{1,2,0:T(2,128)S(1)} all-to-all(f32[16,256,2]{1,2,0:T(2,128)S(1)} %bitcast.72), channel_id=1, replica_groups=mesh['dp'=2,'ei'=4,'eo'=4] {'ei','eo'}, dimensions={0} | all-to-all | bytes 65536 | tf_op jit(solution)/shard_map/all_to_all | solution.py:23
  26.3 64.9 %all-gather.3.cloned.1.call-done = bf16[4096,1024]{0,1:T(8,128)(2,1)} async-done(((bf16[256,1024]{0,1:T(8,128)(2,1)}), bf16[4096,1024]{0,1:T(8,128)(2,1)}) %all-gather.3.cloned.1.call-update) | async-done | bytes 8388624 | tf_op jit(solution)/shard_map/all_gather | solution.py:25
  91.2 11.5 %fusion.23 = f32[4096,512]{1,0:T(8,128)} fusion(bf16[4096,1024]{0,1:T(8,128)(2,1)} %all-gather.3.cloned.1.call-done, pred[4096]{0:T(1024)(128)(4,1)S(1)} %get-tuple-element.32, bf16[2,1024,512]{2,1,0:T(8,128)(2,1)} %param.11), kind=kOutput, calls=%fused_computation.40 | convolution fusion | flops 4299161600 | bytes 17829888 | tf_op jit(solution)/shard_map/dot_general | solution.py:36
  102.8 6.9 %fusion.24 = f32[4096,512]{1,0:T(8,128)} fusion(bf16[4096,1024]{0,1:T(8,128)(2,1)S(1)} %copy-done.5, pred[4096]{0:T(1024)(128)(4,1)S(1)} %get-tuple-element.32, bf16[2,1024,512]{2,1,0:T(8,128)(2,1)S(1)} %copy-done.8), kind=kOutput, calls=%fused_computation.41 | convolution fusion | flops 4299161600 | bytes 17829888 | tf_op jit(solution)/shard_map/dot_general | solution.py:35
  109.6 60.8 %all-gather.5.cloned.1.call-done = bf16[4096,1024]{0,1:T(8,128)(2,1)} async-done(((bf16[256,1024]{0,1:T(8,128)(2,1)}), bf16[4096,1024]{0,1:T(8,128)(2,1)}) %all-gather.5.cloned.1.call-update) | async-done | bytes 8388624 | tf_op jit(solution)/shard_map/all_gather | solution.py:26
  170.4 18.2 %multiply_convert_fusion = (bf16[4096,512]{1,0:T(8,128)(2,1)}, bf16[4096,512]{1,0:T(8,128)(2,1)}, bf16[4096,512]{1,0:T(8,128)(2,1)}) fusion(f32[4096,512]{1,0:T(8,128)} %fusion.24, f32[4096,512]{1,0:T(8,128)} %fusion.23, bf16[2,512,1024]{2,1,0:T(8,128)(2,1)S(1)} %copy-done.6, bf16[4096,1024]{0,1:T(8,128)(2,1)} %all-gather.5.cloned.1.call-done, ...), kind=kOutput, calls=%fused_computation.16 | convolution fusion | flops 4343201792 | bytes 38817792 | tf_op jit(solution)/shard_map/dot_general | solution.py:48
  188.6 9.4 %convolution_convert_fusion = bf16[4096,1024]{0,1:T(8,128)(2,1)} fusion(bf16[4096,512]{1,0:T(8,128)(2,1)} %get-tuple-element.37, bf16[2,512,1024]{2,1,0:T(8,128)(2,1)S(1)} %copy-done.7), kind=kOutput, calls=%fused_computation.28 | convolution fusion | flops 4299161600 | bytes 13631488 | tf_op jit(solution)/shard_map/dot_general | solution.py:39
  198.0 10.8 %fusion.19 = f32[4096,512]{1,0:T(8,128)} fusion(bf16[4096,1024]{0,1:T(8,128)(2,1)} %all-gather.3.cloned.1.call-done, pred[4096]{0:T(1024)(128)(4,1)S(1)} %get-tuple-element.33, bf16[2,1024,512]{2,1,0:T(8,128)(2,1)S(1)} %copy-done.1), kind=kOutput, calls=%fused_computation.36 | convolution fusion | flops 4299161600 | bytes 17829888 | tf_op jit(solution)/shard_map/dot_general | solution.py:36
  208.9 6.9 %fusion.20 = f32[4096,512]{1,0:T(8,128)} fusion(bf16[4096,1024]{0,1:T(8,128)(2,1)S(1)} %bitcast.82, pred[4096]{0:T(1024)(128)(4,1)S(1)} %get-tuple-element.33, bf16[2,1024,512]{2,1,0:T(8,128)(2,1)S(1)} %copy-done.9), kind=kOutput, calls=%fused_computation.37 | convolution fusion | flops 4299161600 | bytes 17829888 | tf_op jit(solution)/shard_map/dot_general | solution.py:35
  215.7 18.0 %multiply_convert_fusion.2 = (bf16[4096,512]{1,0:T(8,128)(2,1)}, bf16[4096,512]{1,0:T(8,128)(2,1)}, bf16[4096,512]{1,0:T(8,128)(2,1)}) fusion(f32[4096,512]{1,0:T(8,128)} %fusion.20, f32[4096,512]{1,0:T(8,128)} %fusion.19, bf16[2,512,1024]{2,1,0:T(8,128)(2,1)S(1)} %copy-done.7, bf16[4096,1024]{0,1:T(8,128)(2,1)} %all-gather.5.cloned.1.call-done, ...), kind=kOutput, calls=%fused_computation.18 | convolution fusion | flops 4343201792 | bytes 38817792 | tf_op jit(solution)/shard_map/dot_general | solution.py:48
  233.8 26.5 %fusion.3 = (f32[4096]{0:T(1024)S(1)}, f32[4096]{0:T(1024)S(1)}, f32[4096,1024]{0,1:T(8,128)}) fusion(bf16[4096,1024]{0,1:T(8,128)(2,1)} %all-gather.5.cloned.1.call-done, bf16[4096,1024]{0,1:T(8,128)(2,1)} %convolution_convert_fusion, f32[4096]{0:T(1024)S(1)} %bitcast.77, f32[4096]{0:T(1024)S(1)} %bitcast.74, bf16[4096,512]{1,0:T(8,128)(2,1)} %get-tuple-element.40, ...), kind=kOutput, calls=%fused_computation.9 | convolution fusion | flops 4341096448 | bytes 38862848 | tf_op jit(solution)/shard_map/dot_general | solution.py:39
  260.4 12.9 %fusion.59 = f32[4096,1024]{1,0:T(8,128)} fusion(bf16[4096,512]{1,0:T(8,128)(2,1)} %get-tuple-element.39, bf16[2,1024,512]{2,1,0:T(8,128)(2,1)} %param.10), kind=kOutput, calls=%fused_computation.75 | convolution fusion | flops 4294967296 | bytes 22020096 | tf_op jit(solution)/shard_map/dot_general | solution.py:51
  273.3 8.2 %fusion.56 = f32[4096,1024]{1,0:T(8,128)} fusion(bf16[4096,512]{1,0:T(8,128)(2,1)S(1)} %copy-done.13, bf16[2,1024,512]{2,1,0:T(8,128)(2,1)S(1)} %copy-done.1), kind=kOutput, calls=%fused_computation.72 | convolution fusion | flops 4294967296 | bytes 22020096 | tf_op jit(solution)/shard_map/dot_general | solution.py:52
  281.5 8.2 %fusion.51 = f32[4096,1024]{1,0:T(8,128)} fusion(bf16[4096,512]{1,0:T(8,128)(2,1)S(1)} %copy-done.11, bf16[2,1024,512]{2,1,0:T(8,128)(2,1)S(1)} %copy-done.10), kind=kOutput, calls=%fused_computation.67 | convolution fusion | flops 4294967296 | bytes 22020096 | tf_op jit(solution)/shard_map/dot_general | solution.py:51
  289.7 24.1 %convert_add_fusion = f32[4096,1024]{1,0:T(8,128)} fusion(f32[4096,1024]{1,0:T(8,128)} %fusion.59, f32[4096,1024]{1,0:T(8,128)} %fusion.56, f32[4096,1024]{1,0:T(8,128)} %fusion.51, bf16[4096,512]{1,0:T(8,128)(2,1)S(1)} %copy-done, bf16[2,1024,512]{2,1,0:T(8,128)(2,1)} %param.11), kind=kOutput, calls=%fused_computation.11 | convolution fusion | flops 4324327424 | bytes 72351744 | tf_op jit(solution)/shard_map/dot_general | solution.py:52
  314.5 3.7 all-to-all-start.1
  318.3 8.3 %fusion.38 = f32[1,1024,512]{2,1,0:T(8,128)S(1)} fusion(bf16[4096,512]{1,0:T(8,128)(2,1)} %get-tuple-element.35, bf16[4096,1024]{0,1:T(8,128)(2,1)} %all-gather.3.cloned.1.call-done, pred[4096]{0:T(1024)(128)(4,1)S(1)} %copy-done.4), kind=kOutput, calls=%fused_computation.58 | convolution fusion | flops 4299161600 | bytes 14684160 | tf_op jit(solution)/shard_map/dot_general | solution.py:58
  326.6 7.1 %fusion.37 = f32[1,1024,512]{2,1,0:T(8,128)S(1)} fusion(bf16[4096,512]{1,0:T(8,128)(2,1)S(1)} %copy-done.12, bf16[4096,1024]{0,1:T(8,128)(2,1)} %all-gather.3.cloned.1.call-done, pred[4096]{0:T(1024)(128)(4,1)S(1)} %copy-done.4), kind=kOutput, calls=%fused_computation.57 | convolution fusion | flops 4299161600 | bytes 14684160 | tf_op jit(solution)/shard_map/dot_general | solution.py:58
  333.7 4.5 fusion.40
  338.2 6.7 %fusion.39 = f32[1,1024,512]{2,1,0:T(8,128)S(1)} fusion(bf16[4096,512]{1,0:T(8,128)(2,1)} %get-tuple-element.39, bf16[4096,1024]{0,1:T(8,128)(2,1)S(1)} %bitcast.84, pred[4096]{0:T(1024)(128)(4,1)S(1)} %get-tuple-element.33), kind=kOutput, calls=%fused_computation.59 | convolution fusion | flops 4299161600 | bytes 14684160 | tf_op jit(solution)/shard_map/dot_general | solution.py:58
  345.0 4.4 pad_maximum_fusion
  349.4 6.9 %fusion.41 = f32[1,512,1024]{2,1,0:T(8,128)S(1)} fusion(bf16[4096,512]{1,0:T(8,128)(2,1)} %get-tuple-element.37, bf16[4096,1024]{0,1:T(8,128)(2,1)S(1)} %bitcast.80, f32[4096]{0:T(1024)S(1)} %bitcast.78, pred[4096]{0:T(1024)(128)(4,1)S(1)} %copy-done.4), kind=kOutput, calls=%fused_computation.61 | convolution fusion | flops 4311744512 | bytes 14700544 | tf_op jit(solution)/shard_map/dot_general | solution.py:58
  356.3 4.5 fusion.44
  360.8 2.5 pad_maximum_fusion.2
  364.0 71.6 %reduce-scatter.3.cloned.1.call-done = f32[256,1024]{0,1:T(8,128)} async-done(((f32[4096,1024]{0,1:T(8,128)}), f32[256,1024]{0,1:T(8,128)}) %reduce-scatter.3.cloned.1.call-update) | async-done | bytes 1048592 | tf_op jit(solution)/shard_map/reduce_scatter | solution.py:43
  435.6 1.3 convert_element_type.71
  436.9 1.0 copy.35
  437.9 176.8 %reduce-scatter.5.cloned.1.call-done = f32[256,1024]{1,0:T(8,128)} async-done(((f32[4096,1024]{1,0:T(8,128)}), f32[256,1024]{1,0:T(8,128)}) %reduce-scatter.5.cloned.1.call-update) | async-done | bytes 1048592 | tf_op jit(solution)/shard_map/reduce_scatter | solution.py:55
  614.7 2.1 convert_element_type.83
  (65 shorter events, 1.8 us)
Async XLA Ops:
  7.2 84.0 %all-gather.3.cloned.1.call-start = ((), (), s32[]{:S(2)}) async-start(), calls=%async_computation.4 | async-start | bytes 8912896 | tf_op jit(solution)/shard_map/all_gather | solution.py:25
  9.3 161.2 %all-gather.5.cloned.1.call-start = ((), (), s32[]{:S(2)}) async-start(), calls=%async_computation.6 | async-start | bytes 8912896 | tf_op jit(solution)/shard_map/all_gather | solution.py:26
  11.4 424.2 %reduce-scatter.3.cloned.1.call-start = ((), (), s32[]{:S(2)}) async-start(), calls=%async_computation.5 | async-start | bytes 17825792 | tf_op jit(solution)/shard_map/reduce_scatter | solution.py:43
  26.2 144.2 %copy-start.3 = (pred[4096]{0:T(1024)(128)(4,1)}, pred[4096]{0:T(1024)(128)(4,1)S(1)}, u32[]{:S(2)}) copy-start(pred[4096]{0:T(1024)(128)(4,1)S(1)} %get-tuple-element.32) | copy-start | bytes 12292
  91.2 11.6 %copy-start.5 = (bf16[4096,1024]{0,1:T(8,128)(2,1)S(1)}, bf16[4096,1024]{0,1:T(8,128)(2,1)}, u32[]{:S(2)}) copy-start(bf16[4096,1024]{0,1:T(8,128)(2,1)} %all-gather.3.cloned.1.call-done) | copy-start | bytes 25165828
  91.2 11.6 %copy-start.8 = (bf16[2,1024,512]{2,1,0:T(8,128)(2,1)S(1)}, bf16[2,1024,512]{2,1,0:T(8,128)(2,1)}, u32[]{:S(2)}) copy-start(bf16[2,1024,512]{2,1,0:T(8,128)(2,1)} %param.10) | copy-start | bytes 6291460
  102.8 67.7 %copy-start.6 = (bf16[2,512,1024]{2,1,0:T(8,128)(2,1)S(1)}, bf16[2,512,1024]{2,1,0:T(8,128)(2,1)}, u32[]{:S(2)}) copy-start(bf16[2,512,1024]{2,1,0:T(8,128)(2,1)} %param.12) | copy-start | bytes 6291460
  170.4 18.2 %copy-start.7 = (bf16[2,512,1024]{2,1,0:T(8,128)(2,1)S(1)}, bf16[2,512,1024]{2,1,0:T(8,128)(2,1)}, u32[]{:S(2)}) copy-start(bf16[2,512,1024]{2,1,0:T(8,128)(2,1)} %param.12) | copy-start | bytes 6291460
  188.6 9.4 %copy-start.1 = (bf16[2,1024,512]{2,1,0:T(8,128)(2,1)S(1)}, bf16[2,1024,512]{2,1,0:T(8,128)(2,1)}, u32[]{:S(2)}) copy-start(bf16[2,1024,512]{2,1,0:T(8,128)(2,1)} %param.11) | copy-start | bytes 6291460
  188.6 20.3 %slice-start.2 = ((s8[8388608]{0:T(1024)(128)(4,1)}), s8[4194304]{0:T(1024)(128)(4,1)S(1)}, s32[]{:S(2)}) async-start(s8[8388608]{0:T(1024)(128)(4,1)} %bitcast.81), calls=%async_computation.10 | async-start | bytes 8388608
  198.0 10.8 %slice-start.3 = ((s8[8388608]{0:T(1024)(128)(4,1)}), s8[4194304]{0:T(1024)(128)(4,1)S(1)}, s32[]{:S(2)}) async-start(s8[8388608]{0:T(1024)(128)(4,1)} %bitcast.81), calls=%async_computation.11 | async-start | bytes 8388608
  198.0 10.8 %copy-start.9 = (bf16[2,1024,512]{2,1,0:T(8,128)(2,1)S(1)}, bf16[2,1024,512]{2,1,0:T(8,128)(2,1)}, u32[]{:S(2)}) copy-start(bf16[2,1024,512]{2,1,0:T(8,128)(2,1)} %param.10) | copy-start | bytes 6291460
  260.3 354.4 %reduce-scatter.5.cloned.1.call-start = ((), (), s32[]{:S(2)}) async-start(), calls=%async_computation.7 | async-start | bytes 17825792 | tf_op jit(solution)/shard_map/reduce_scatter | solution.py:55
  260.4 12.9 %copy-start.13 = (bf16[4096,512]{1,0:T(8,128)(2,1)S(1)}, bf16[4096,512]{1,0:T(8,128)(2,1)}, u32[]{:S(2)}) copy-start(bf16[4096,512]{1,0:T(8,128)(2,1)} %get-tuple-element.38) | copy-start | bytes 12582916
  273.3 8.2 %copy-start.10 = (bf16[2,1024,512]{2,1,0:T(8,128)(2,1)S(1)}, bf16[2,1024,512]{2,1,0:T(8,128)(2,1)}, u32[]{:S(2)}) copy-start(bf16[2,1024,512]{2,1,0:T(8,128)(2,1)} %param.10) | copy-start | bytes 6291460
  273.3 8.2 %copy-start.11 = (bf16[4096,512]{1,0:T(8,128)(2,1)S(1)}, bf16[4096,512]{1,0:T(8,128)(2,1)}, u32[]{:S(2)}) copy-start(bf16[4096,512]{1,0:T(8,128)(2,1)} %get-tuple-element.36) | copy-start | bytes 12582916
  281.5 8.2 %copy-start = (bf16[4096,512]{1,0:T(8,128)(2,1)S(1)}, bf16[4096,512]{1,0:T(8,128)(2,1)}, u32[]{:S(2)}) copy-start(bf16[4096,512]{1,0:T(8,128)(2,1)} %get-tuple-element.35) | copy-start | bytes 12582916
  313.8 4.4 copy-start.4
  314.5 48.8 %all-to-all-start.1 = ((f32[16,256,2]{1,2,0:T(2,128)}), f32[16,256,2]{1,2,0:T(2,128)S(1)}, u32[]{:S(2)}, u32[]{:S(2)}) async-start(f32[16,256,2]{1,2,0:T(2,128)} %copy.34), calls=%async_computation.3 | async-start | bytes 65536 | tf_op jit(solution)/shard_map/all_to_all | solution.py:64
  318.3 8.3 %copy-start.12 = (bf16[4096,512]{1,0:T(8,128)(2,1)S(1)}, bf16[4096,512]{1,0:T(8,128)(2,1)}, u32[]{:S(2)}) copy-start(bf16[4096,512]{1,0:T(8,128)(2,1)} %get-tuple-element.36) | copy-start | bytes 12582916
  318.3 15.4 %slice-start.4 = ((s8[8388608]{0:T(1024)(128)(4,1)}), s8[4194304]{0:T(1024)(128)(4,1)S(1)}, s32[]{:S(2)}) async-start(s8[8388608]{0:T(1024)(128)(4,1)} %bitcast.83), calls=%async_computation.12 | async-start | bytes 8388608
  326.6 7.1 %slice-start.5 = ((s8[8388608]{0:T(1024)(128)(4,1)}), s8[4194304]{0:T(1024)(128)(4,1)S(1)}, s32[]{:S(2)}) async-start(s8[8388608]{0:T(1024)(128)(4,1)} %bitcast.83), calls=%async_computation.13 | async-start | bytes 8388608
  326.6 7.1 %copy-start.14 = (bf16[4096,512]{1,0:T(8,128)(2,1)S(1)}, bf16[4096,512]{1,0:T(8,128)(2,1)}, u32[]{:S(2)}) copy-start(bf16[4096,512]{1,0:T(8,128)(2,1)} %get-tuple-element.38) | copy-start | bytes 12582916
  333.7 15.6 %slice-start = ((s8[8388608]{0:T(1024)(128)(4,1)}), s8[4194304]{0:T(1024)(128)(4,1)S(1)}, s32[]{:S(2)}) async-start(s8[8388608]{0:T(1024)(128)(4,1)} %bitcast.79), calls=%async_computation.8 | async-start | bytes 8388608
  338.2 11.1 %slice-start.1 = ((s8[8388608]{0:T(1024)(128)(4,1)}), s8[4194304]{0:T(1024)(128)(4,1)S(1)}, s32[]{:S(2)}) async-start(s8[8388608]{0:T(1024)(128)(4,1)} %bitcast.79), calls=%async_computation.9 | async-start | bytes 8388608
  349.3 6.9 %copy-start.15 = (bf16[4096,512]{1,0:T(8,128)(2,1)S(1)}, bf16[4096,512]{1,0:T(8,128)(2,1)}, u32[]{:S(2)}) copy-start(bf16[4096,512]{1,0:T(8,128)(2,1)} %get-tuple-element.40) | copy-start | bytes 12582916
  360.8 2.6 copy-start.2
Sparse Core Ops, SparseCore 0:
  10.7 80.4 all-gather.2
  93.9 76.4 all-gather.4
  260.4 175.1 reduce-scatter.2
  439.6 175.1 reduce-scatter.4

commit v2 on v1

v2 whole, which is shorter than its diff:
```python
import functools

import jax
import jax.numpy as jnp
from jax import lax
from jax.experimental import pallas as pl
from jax.experimental.pallas import tpu as pltpu
from jax.sharding import PartitionSpec as P

MESH = pl.DeviceIdType.MESH
F32 = jnp.float32
BF16 = jnp.bfloat16
SLOTS = 3


def mm(p, q, cp, cq):
    return lax.dot_general(p, q, (((cp,), (cq,)), ((), ())), preferred_element_type=F32)


def ring_kernel(n_z, x_ref, dy_ref, idx_ref, gate_ref, wg_ref, wu_ref, wd_ref,
                y_ref, dx_ref, dgate_ref, dwg_ref, dwu_ref, dwd_ref,
                xd, gt, acc, dga, part, final, dgp, dgf, wg, wu, wd, awg, awu, awd,
                load_sem, xd_send, xd_recv, gt_send, gt_recv, y_send, y_recv, dx_send, dx_recv, dg_send, dg_recv,
                credit):
    tok, top_k = idx_ref.shape
    half = tok // 2
    exp_local = wg_ref.shape[0]
    n_q = 2 * n_z
    n = 2 * n_q
    experts = exp_local * n
    z = lax.axis_index('ei')
    eo = lax.axis_index('eo')
    ycoord, core = eo // 2, eo % 2
    q = z + ycoord * (n_q - 1 - 2 * z)
    me = 2 * q + core
    first_expert = (z * 4 + eo) * exp_local

    def device_at(pos):
        pos = lax.rem(pos + 2 * n, n)
        chip, c = pos // 2, pos % 2
        col = chip // n_z
        return {'ei': chip + col * (n_q - 1 - 2 * chip), 'eo': col * 2 + c}

    right, left = device_at(me + 1), device_at(me - 1)
    to = (right, left)
    back = (left, right)

    loads = [pltpu.make_async_copy(src, dst, load_sem.at[i]) for i, (src, dst) in enumerate(
        ((x_ref, xd.at[0, 0]), (dy_ref, xd.at[0, 1]), (wg_ref, wg), (wu_ref, wu), (wd_ref, wd)))]
    for c in loads:
        c.start()

    barrier = pltpu.get_barrier_semaphore()
    for nb in (left, right):
        pl.semaphore_signal(barrier, inc=1, device_id=nb, device_id_type=MESH)

    lane = lax.broadcasted_iota(jnp.int32, (tok, 128), 1)
    dense = jnp.zeros((tok, 128), F32)
    for j in range(top_k):
        dense = dense + jnp.where(lane == idx_ref[:, j:j + 1], gate_ref[:, j:j + 1], 0.0)
    for d in range(2):
        gt[0, d] = dense[d * half:(d + 1) * half].T[:experts]
    for e in range(exp_local):
        awg[e] = jnp.zeros(awg.shape[1:], F32)
        awu[e] = jnp.zeros(awu.shape[1:], F32)
        awd[e] = jnp.zeros(awd.shape[1:], F32)

    pl.semaphore_wait(barrier, 2)
    loads[0].wait()
    loads[1].wait()

    def rows(d):
        return pl.ds(d * half, half)

    def xd_copy(s, d):
        return pltpu.make_async_remote_copy(
            src_ref=xd.at[s, :, rows(d)], dst_ref=xd.at[s + 1, :, rows(d)], send_sem=xd_send.at[s, d],
            recv_sem=xd_recv.at[s, d], device_id=to[d], device_id_type=MESH)

    def gt_copy(s, d):
        return pltpu.make_async_remote_copy(
            src_ref=gt.at[s, d], dst_ref=gt.at[s + 1, d], send_sem=gt_send.at[s, d],
            recv_sem=gt_recv.at[s, d], device_id=to[d], device_id_type=MESH)

    def acc_copy(s, d, k):
        send, recv = ((y_send, y_recv), (dx_send, dx_recv))[k]
        return pltpu.make_async_remote_copy(
            src_ref=acc.at[lax.rem(s, SLOTS), k, rows(d)], dst_ref=acc.at[lax.rem(s + 1, SLOTS), k, rows(d)],
            send_sem=send.at[s, d], recv_sem=recv.at[s, d], device_id=to[d], device_id_type=MESH)

    def dg_copy(s, d):
        return pltpu.make_async_remote_copy(
            src_ref=dga.at[lax.rem(s, SLOTS), d], dst_ref=dga.at[lax.rem(s + 1, SLOTS), d],
            send_sem=dg_send.at[s, d], recv_sem=dg_recv.at[s, d], device_id=to[d], device_id_type=MESH)

    def compute(s):
        wide = [jnp.concatenate([gt[s, d], jnp.zeros((128 - experts, half), F32)], axis=0).T for d in range(2)]
        gates = jnp.concatenate(wide, axis=0)

        def one(e, carry):
            dgs = carry
            lane_t = lax.broadcasted_iota(jnp.int32, (tok, 128), 1)
            mine = lane_t == first_expert + e
            gcol = jnp.sum(jnp.where(mine, gates, 0.0), axis=1, keepdims=True)
            routed = gcol > 0.0
            x = xd[s, 0]
            a = mm(x, wg[e], 1, 0)
            b = mm(x, wu[e], 1, 0)
            sig = jax.nn.sigmoid(a)
            silu = a * sig
            h = jnp.where(routed, silu * b, 0.0).astype(BF16)
            o = mm(h, wd[e], 1, 0).astype(BF16).astype(F32)
            dyf = xd[s, 1].astype(F32)
            part[0] = jnp.where(e == 0, 0.0, part[0]) + gcol * o
            dg = jnp.sum(dyf * o, axis=1, keepdims=True)
            dgs = dgs + jnp.where(mine, dg, 0.0)
            g = (gcol * dyf).astype(BF16)
            awd[e] = awd[e] + mm(h, g, 0, 0)
            dh = mm(g, wd[e], 1, 1)
            da = jnp.where(routed, dh * b * sig * (1.0 + a * (1.0 - sig)), 0.0).astype(BF16)
            db = jnp.where(routed, dh * silu, 0.0).astype(BF16)
            awg[e] = awg[e] + mm(x, da, 0, 0)
            awu[e] = awu[e] + mm(x, db, 0, 0)
            dxr = (mm(da, wg[e], 1, 1) + mm(db, wu[e], 1, 1)).astype(BF16).astype(F32)
            part[1] = jnp.where(e == 0, 0.0, part[1]) + dxr
            return dgs

        dgs = lax.fori_loop(0, exp_local, one, jnp.zeros((tok, 128), F32))
        for d in range(2):
            dgp[d] = dgs[d * half:(d + 1) * half].T[:experts]

    for c in loads[2:]:
        c.wait()

    def step(s, carry):
        slot = lax.rem(s, SLOTS)

        @pl.when(s >= 1)
        def _():
            for d in range(2):
                xd_copy(s - 1, d).wait_recv()
                gt_copy(s - 1, d).wait_recv()

        @pl.when(s <= n - 2)
        def _():
            for d in range(2):
                gt_copy(s, d).start()
                xd_copy(s, d).start()

        compute(s)

        @pl.when(s >= 2)
        def _():
            for d in range(2):
                for k in range(2):
                    acc_copy(s - 1, d, k).wait_send()
                dg_copy(s - 1, d).wait_send()

        @pl.when(jnp.logical_and(s >= 2, s - 1 + SLOTS <= n))
        def _():
            for d in range(2):
                pl.semaphore_signal(credit.at[d], inc=1, device_id=back[d], device_id_type=MESH)

        @pl.when(s == 0)
        def _():
            final[...] = part[...]
            dgf[...] = dgp[...]

        @pl.when(jnp.logical_and(s >= 1, s + 1 - SLOTS >= 1))
        def _():
            for d in range(2):
                pl.semaphore_wait(credit.at[d], 1)

        @pl.when(s == 1)
        def _():
            acc[slot] = part[...]
            dga[slot] = dgp[...]
            for d in range(2):
                for k in range(2):
                    acc_copy(s, d, k).start()
                dg_copy(s, d).start()

        @pl.when(s >= 2)
        def _():
            for k in range(2):
                for d in range(2):
                    acc_copy(s - 1, d, k).wait_recv()
                    acc[slot, k, rows(d)] = acc[slot, k, rows(d)] + part[k, rows(d)]
                    acc_copy(s, d, k).start()
            for d in range(2):
                dg_copy(s - 1, d).wait_recv()
                dga[slot, d] = dga[slot, d] + dgp[d]
                dg_copy(s, d).start()

        @pl.when(s >= 1)
        def _():
            for d in range(2):
                xd_copy(s - 1, d).wait_send()
                gt_copy(s - 1, d).wait_send()

        return carry

    lax.fori_loop(0, n, step, 0)

    stores = [pltpu.make_async_copy(src, dst, load_sem.at[i]) for i, (src, dst) in enumerate(
        ((awg, dwg_ref), (awu, dwu_ref), (awd, dwd_ref)))]
    for c in stores:
        c.start()
    last = n % SLOTS
    for d in range(2):
        for k in range(2):
            acc_copy(n - 1, d, k).wait_send()
        dg_copy(n - 1, d).wait_send()
    for d in range(2):
        for k in range(2):
            acc_copy(n - 1, d, k).wait_recv()
        dg_copy(n - 1, d).wait_recv()
    y_ref[...] = (acc[last, 0] + final[0]).astype(BF16)
    dx_ref[...] = (acc[last, 1] + final[1]).astype(BF16)
    cols = []
    for d in range(2):
        cols.append(jnp.concatenate([dga[last, d] + dgf[d], jnp.zeros((128 - experts, half), F32)], axis=0).T)
    dg_all = jnp.concatenate(cols, axis=0)
    for j in range(top_k):
        dgate_ref[:, j:j + 1] = jnp.sum(jnp.where(lane == idx_ref[:, j:j + 1], dg_all, 0.0), axis=1, keepdims=True)
    for c in stores:
        c.wait()


def solution(mesh):
    n_z = mesh.shape['ei']
    n = n_z * mesh.shape['eo']
    tok_spec = P(('dp', 'ei', 'eo'), None)
    weight_spec = P(('ei', 'eo'), None, None)
    grad_spec = P(('dp', 'ei', 'eo'), None, None)

    def device_layer(x_loc, idx_loc, gate_loc, wg_loc, wu_loc, wd_loc, dy_loc):
        tok, top_k = idx_loc.shape
        d_model = x_loc.shape[1]
        exp_local, _, ff = wg_loc.shape
        experts = exp_local * n
        half = tok // 2
        hbm = pl.BlockSpec(memory_space=pl.ANY)
        vm = pl.BlockSpec(memory_space=pltpu.VMEM)
        dma = pltpu.SemaphoreType.DMA
        y, dx, dgate, dwg, dwu, dwd = pl.pallas_call(
            functools.partial(ring_kernel, n_z),
            out_shape=(jax.ShapeDtypeStruct((tok, d_model), BF16), jax.ShapeDtypeStruct((tok, d_model), BF16),
                       jax.ShapeDtypeStruct((tok, top_k), F32), jax.ShapeDtypeStruct(wg_loc.shape, F32),
                       jax.ShapeDtypeStruct(wu_loc.shape, F32), jax.ShapeDtypeStruct(wd_loc.shape, F32)),
            in_specs=[hbm, hbm, vm, vm, hbm, hbm, hbm],
            out_specs=(vm, vm, vm, hbm, hbm, hbm),
            scratch_shapes=[
                pltpu.VMEM((n, 2, tok, d_model), BF16),
                pltpu.VMEM((n, 2, experts, half), F32),
                pltpu.VMEM((SLOTS, 2, tok, d_model), F32),
                pltpu.VMEM((SLOTS, 2, experts, half), F32),
                pltpu.VMEM((2, tok, d_model), F32),
                pltpu.VMEM((2, tok, d_model), F32),
                pltpu.VMEM((2, experts, half), F32),
                pltpu.VMEM((2, experts, half), F32),
                pltpu.VMEM(wg_loc.shape, BF16), pltpu.VMEM(wu_loc.shape, BF16), pltpu.VMEM(wd_loc.shape, BF16),
                pltpu.VMEM(wg_loc.shape, F32), pltpu.VMEM(wu_loc.shape, F32), pltpu.VMEM(wd_loc.shape, F32),
                dma((5,)),
                dma((n, 2)), dma((n, 2)), dma((n, 2)), dma((n, 2)), dma((n, 2)), dma((n, 2)),
                dma((n, 2)), dma((n, 2)), dma((n, 2)), dma((n, 2)),
                pltpu.SemaphoreType.REGULAR((2,)),
            ],
            compiler_params=pltpu.CompilerParams(collective_id=0, has_side_effects=True, vmem_limit_bytes=60 * 1024 * 1024),
        )(x_loc, dy_loc, idx_loc, gate_loc, wg_loc, wu_loc, wd_loc)
        return y, dx, dgate, dwg, dwu, dwd

    return jax.shard_map(device_layer, mesh=mesh, in_specs=(tok_spec, tok_spec, tok_spec, weight_spec, weight_spec, weight_spec, tok_spec), out_specs=(tok_spec, tok_spec, tok_spec, grad_spec, grad_spec, grad_spec), check_vma=False)
```

time: 633 us -> 294 us (0.46); the launches traced: 624 us -> 293 us
  waiting for transfers between devices: 374 us -> 0 us
  Pallas kernels: 0 us -> 274 us
  matrix products: 200 us -> 0 us
  blocking collectives: 13.9 us -> 0 us
  between operations: 14.5 us -> 0.65 us
  local copies, waits for them, and re-layouts: 5.91 us -> 18.8 us
  other arithmetic: 11.8 us -> 0 us
    pallas_call x0 -> x1, Pallas kernels: none -> 274 us  [device_layer(): pl.pallas_call(functools.partial(ring_kernel, n_z), out_shape=(jax.ShapeD...]
    reduce_scatter x2 -> x0, waiting for transfers between devices: 248 us -> none  [the longest x1 177 us: device_layer(): lax.psum_scatter(dx_part, GROUP, scatter_dimension=0, tiled=True)]
    dot_general x18 -> x0, matrix products: 200 us -> none  [the longest x6 38 us: tdot(): lax.dot_general(p, q, (((0,), (0,)), ((), ())), preferred_element_type=jn...]
    all_gather x2 -> x0, waiting for transfers between devices: 126 us -> none  [the longest x1 64.9 us: device_layer(): x_all = lax.all_gather(x_loc, GROUP, axis=0, tiled=True)]
    all_to_all x1 -> x0, blocking collectives: 13.9 us -> none  [device_layer(): lax.all_to_all(dense_gate.reshape(tok_count, group_devs, exp_local).trans...]
    unnamed x47 -> x11, local copies, waits for them, and re-layouts: 5.18 us -> 17.2 us
    another operation x3 -> x0, other arithmetic: 6.92 us -> none  [the longest x1 4.37 us: device_layer(): dw_gate = jnp.stack([tdot(x_e, da) for x_e, da, db, h, g in grads])]
  transfers between devices with their start and end apart: 5 -> 0, of which waited for: 4 -> 0; matrix products, arithmetic and copies ran while one was open for 20% -> 0% of each run, Pallas kernels for 0% -> 0%
where the time goes in v2:
time: 294 us; the launch traced here: 293 us
  Pallas kernels  274 us (93%)
  local copies, waits for them, and re-layouts  18.8 us (6%)
    pallas_call x1, Pallas kernels, device_layer(): pl.pallas_call(functools.partial(ring_kernel, n_z), out_shape=(jax.ShapeD...  274 us
    unnamed x11, local copies, waits for them, and re-layouts  17.2 us

profile of v2, /device:TPU:0, one launch (start us, length us, event | category | flops | bytes accessed | tf_op | source)
XLA Modules:
  0.0 293.5 jit_solution(1263461514658458300)
XLA Ops:
  0.6 1.5 copy.13.idx_ref
  2.1 1.5 copy.14.gate_ref
  3.6 274.0 %shard_map.118 = (bf16[256,1024]{1,0:T(8,128)(2,1)}, bf16[256,1024]{1,0:T(8,128)(2,1)}, f32[256,8]{1,0:T(8,128)}, f32[2,1024,512]{2,1,0:T(8,128)}, f32[2,1024,512]{2,1,0:T(8,128)}, /*index=5*/f32[2,512,1024]{2,1,0:T(8,128)}) custom-call(bf16[256,1024]{1,0:T(8,128)(2,1)} %x_ref.1, bf16[256,1024]{1,0:T(8,128)(2,1)} %dy_ref.1, s32[256,8]{1,0:T(8,128)} %copy.13.idx_ref, ...), custom_call_target="tpu_custom_call" | custom-call | tf_op jit(solution)/shard_map/pallas_call | solution.py:246
  277.6 1.6 copy.15
  279.2 1.9 copy.21
  281.1 1.9 copy.22
  282.9 0.0 copy-start.1
  282.9 4.8 %copy.23 = f32[2,1024,512]{2,1,0:T(8,128)} copy(f32[2,1024,512]{2,1,0:T(8,128)} %get-tuple-element.21) | data formatting | bytes 8388608
  287.7 0.0 copy-done.1
  287.7 0.0 copy-start
  287.7 2.1 copy.24
  289.9 1.6 copy-done
  291.4 2.0 copy.25
Async XLA Ops:
  282.9 4.8 %copy-start.1 = (f32[2,1024,512]{2,1,0:T(8,128)S(1)}, f32[2,1024,512]{2,1,0:T(8,128)}, u32[]{:S(2)}) copy-start(f32[2,1024,512]{2,1,0:T(8,128)} %get-tuple-element.22) | copy-start | bytes 12582916
  287.7 3.7 %copy-start = (f32[2,512,1024]{2,1,0:T(8,128)S(1)}, f32[2,512,1024]{2,1,0:T(8,128)}, u32[]{:S(2)}) copy-start(f32[2,512,1024]{2,1,0:T(8,128)} %get-tuple-element.23) | copy-start | bytes 12582916

commit v3 on v2

--- a/solution.py
+++ b/solution.py
@@ -18,11 +18,10 @@
 
 
 def ring_kernel(n_z, x_ref, dy_ref, idx_ref, gate_ref, wg_ref, wu_ref, wd_ref,
-                y_ref, dx_ref, dgate_ref, dwg_ref, dwu_ref, dwd_ref,
-                xd, gt, acc, dga, part, final, dgp, dgf, wg, wu, wd, awg, awu, awd,
-                load_sem, xd_send, xd_recv, gt_send, gt_recv, y_send, y_recv, dx_send, dx_recv, dg_send, dg_recv,
-                credit):
-    tok, top_k = idx_ref.shape
+                y_ref, dx_ref, dgate_ref, awg, awu, awd,
+                xd, gt, acc, dga, part, dgp, pb, dgb, wg, wu, wd,
+                load_sem, xd_send, xd_recv, gt_send, gt_recv, y_send, y_recv, dx_send, dx_recv, dg_send, dg_recv, pb_recv, credit):
+    top_k, tok = idx_ref.shape
     half = tok // 2
     exp_local = wg_ref.shape[0]
     n_q = 2 * n_z
@@ -44,6 +43,8 @@
     right, left = device_at(me + 1), device_at(me - 1)
     to = (right, left)
     back = (left, right)
+    partner = {'ei': z, 'eo': eo + 1 - 2 * core}
+    leaves = (core == 1, core == 0)
 
     loads = [pltpu.make_async_copy(src, dst, load_sem.at[i]) for i, (src, dst) in enumerate(
         ((x_ref, xd.at[0, 0]), (dy_ref, xd.at[0, 1]), (wg_ref, wg), (wu_ref, wu), (wd_ref, wd)))]
@@ -54,12 +55,12 @@
     for nb in (left, right):
         pl.semaphore_signal(barrier, inc=1, device_id=nb, device_id_type=MESH)
 
-    lane = lax.broadcasted_iota(jnp.int32, (tok, 128), 1)
-    dense = jnp.zeros((tok, 128), F32)
+    row = lax.broadcasted_iota(jnp.int32, (experts, tok), 0)
+    dense = jnp.zeros((experts, tok), F32)
     for j in range(top_k):
-        dense = dense + jnp.where(lane == idx_ref[:, j:j + 1], gate_ref[:, j:j + 1], 0.0)
-    for d in range(2):
-        gt[0, d] = dense[d * half:(d + 1) * half].T[:experts]
+        dense = dense + jnp.where(row == idx_ref[j:j + 1, :], gate_ref[j:j + 1, :], 0.0)
+    for d in range(2):
+        gt[0, d] = dense[:, d * half:(d + 1) * half]
     for e in range(exp_local):
         awg[e] = jnp.zeros(awg.shape[1:], F32)
         awu[e] = jnp.zeros(awu.shape[1:], F32)
@@ -92,6 +93,26 @@
         return pltpu.make_async_remote_copy(
             src_ref=dga.at[lax.rem(s, SLOTS), d], dst_ref=dga.at[lax.rem(s + 1, SLOTS), d],
             send_sem=dg_send.at[s, d], recv_sem=dg_recv.at[s, d], device_id=to[d], device_id_type=MESH)
+
+    def xd_direct(d):
+        return pltpu.make_async_remote_copy(
+            src_ref=xd.at[0, :, rows(d)], dst_ref=xd.at[n - 1, :, rows(d)], send_sem=xd_send.at[n - 2, d],
+            recv_sem=xd_recv.at[n - 2, d], device_id=partner, device_id_type=MESH)
+
+    def gt_direct(d):
+        return pltpu.make_async_remote_copy(
+            src_ref=gt.at[0, d], dst_ref=gt.at[n - 1, d], send_sem=gt_send.at[n - 2, d],
+            recv_sem=gt_recv.at[n - 2, d], device_id=partner, device_id_type=MESH)
+
+    def pb_copy(d, k):
+        return pltpu.make_async_remote_copy(
+            src_ref=acc.at[1, k, rows(d)], dst_ref=pb.at[k], send_sem=(y_send, dx_send)[k].at[1, d],
+            recv_sem=pb_recv.at[k], device_id=partner, device_id_type=MESH)
+
+    def dgb_copy(d):
+        return pltpu.make_async_remote_copy(
+            src_ref=dga.at[1, d], dst_ref=dgb, send_sem=dg_send.at[1, d],
+            recv_sem=pb_recv.at[2], device_id=partner, device_id_type=MESH)
 
     def compute(s):
         wide = [jnp.concatenate([gt[s, d], jnp.zeros((128 - experts, half), F32)], axis=0).T for d in range(2)]
@@ -129,21 +150,26 @@
         for d in range(2):
             dgp[d] = dgs[d * half:(d + 1) * half].T[:experts]
 
+    for d in range(2):
+        gt_copy(0, d).start()
+        xd_copy(0, d).start()
+    for d in range(2):
+        @pl.when(leaves[d])
+        def _(d=d):
+            gt_direct(d).start()
+            xd_direct(d).start()
+
     for c in loads[2:]:
         c.wait()
 
     def step(s, carry):
         slot = lax.rem(s, SLOTS)
-
-        @pl.when(s >= 1)
-        def _():
-            for d in range(2):
-                xd_copy(s - 1, d).wait_recv()
-                gt_copy(s - 1, d).wait_recv()
-
-        @pl.when(s <= n - 2)
-        def _():
-            for d in range(2):
+        for d in range(2):
+            xd_copy(s - 1, d).wait_recv()
+            gt_copy(s - 1, d).wait_recv()
+        for d in range(2):
+            @pl.when(jnp.logical_or(s < n - 2, jnp.logical_and(s == n - 2, jnp.logical_not(leaves[d]))))
+            def _(d=d):
                 gt_copy(s, d).start()
                 xd_copy(s, d).start()
 
@@ -161,70 +187,71 @@
             for d in range(2):
                 pl.semaphore_signal(credit.at[d], inc=1, device_id=back[d], device_id_type=MESH)
 
-        @pl.when(s == 0)
+        @pl.when(s >= SLOTS)
         def _():
-            final[...] = part[...]
-            dgf[...] = dgp[...]
-
-        @pl.when(jnp.logical_and(s >= 1, s + 1 - SLOTS >= 1))
-        def _():
             for d in range(2):
                 pl.semaphore_wait(credit.at[d], 1)
 
-        @pl.when(s == 1)
-        def _():
-            acc[slot] = part[...]
-            dga[slot] = dgp[...]
-            for d in range(2):
+        for d in range(2):
+            fresh = jnp.logical_or(s == 1, jnp.logical_and(s == 2, jnp.logical_not(leaves[d])))
+
+            @pl.when(fresh)
+            def _(d=d):
+                acc[slot, :, rows(d)] = part[:, rows(d)]
+                dga[slot, d] = dgp[d]
+
+            @pl.when(jnp.logical_and(s == 1, leaves[d]))
+            def _(d=d):
+                for k in range(2):
+                    pb_copy(d, k).start()
+                dgb_copy(d).start()
+
+            @pl.when(jnp.logical_and(fresh, jnp.logical_not(jnp.logical_and(s == 1, leaves[d]))))
+            def _(d=d):
                 for k in range(2):
                     acc_copy(s, d, k).start()
                 dg_copy(s, d).start()
 
-        @pl.when(s >= 2)
-        def _():
-            for k in range(2):
-                for d in range(2):
+        for k in range(2):
+            for d in range(2):
+                @pl.when(jnp.logical_or(s >= 3, jnp.logical_and(s == 2, leaves[d])))
+                def _(d=d, k=k):
                     acc_copy(s - 1, d, k).wait_recv()
                     acc[slot, k, rows(d)] = acc[slot, k, rows(d)] + part[k, rows(d)]
                     acc_copy(s, d, k).start()
-            for d in range(2):
-                dg_copy(s - 1, d).wait_recv()
-                dga[slot, d] = dga[slot, d] + dgp[d]
-                dg_copy(s, d).start()
-
-        @pl.when(s >= 1)
-        def _():
-            for d in range(2):
-                xd_copy(s - 1, d).wait_send()
-                gt_copy(s - 1, d).wait_send()
+                    if k == 1:
+                        dg_copy(s - 1, d).wait_recv()
+                        dga[slot, d] = dga[slot, d] + dgp[d]
+                        dg_copy(s, d).start()
+
+        for d in range(2):
+            xd_copy(s - 1, d).wait_send()
+            gt_copy(s - 1, d).wait_send()
 
         return carry
 
-    lax.fori_loop(0, n, step, 0)
-
-    stores = [pltpu.make_async_copy(src, dst, load_sem.at[i]) for i, (src, dst) in enumerate(
-        ((awg, dwg_ref), (awu, dwu_ref), (awd, dwd_ref)))]
-    for c in stores:
-        c.start()
+    lax.fori_loop(1, n, step, 0)
+
+    compute(0)
     last = n % SLOTS
     for d in range(2):
         for k in range(2):
             acc_copy(n - 1, d, k).wait_send()
         dg_copy(n - 1, d).wait_send()
+    for k in range(2):
+        pb_copy(0, k).wait_recv()
+    dgb_copy(0).wait_recv()
+    dgs = []
     for d in range(2):
         for k in range(2):
             acc_copy(n - 1, d, k).wait_recv()
+            out = (y_ref, dx_ref)[k]
+            out[rows(d)] = (acc[last, k, rows(d)] + part[k, rows(d)] + jnp.where(leaves[d], 0.0, pb[k])).astype(BF16)
         dg_copy(n - 1, d).wait_recv()
-    y_ref[...] = (acc[last, 0] + final[0]).astype(BF16)
-    dx_ref[...] = (acc[last, 1] + final[1]).astype(BF16)
-    cols = []
-    for d in range(2):
-        cols.append(jnp.concatenate([dga[last, d] + dgf[d], jnp.zeros((128 - experts, half), F32)], axis=0).T)
-    dg_all = jnp.concatenate(cols, axis=0)
+        dgs.append(dga[last, d] + dgp[d] + jnp.where(leaves[d], 0.0, dgb[...]))
+    dg_all = jnp.concatenate(dgs, axis=1)
     for j in range(top_k):
-        dgate_ref[:, j:j + 1] = jnp.sum(jnp.where(lane == idx_ref[:, j:j + 1], dg_all, 0.0), axis=1, keepdims=True)
-    for c in stores:
-        c.wait()
+        dgate_ref[j:j + 1, :] = jnp.sum(jnp.where(row == idx_ref[j:j + 1, :], dg_all, 0.0), axis=0, keepdims=True)
 
 
 def solution(mesh):
@@ -243,31 +270,30 @@
         hbm = pl.BlockSpec(memory_space=pl.ANY)
         vm = pl.BlockSpec(memory_space=pltpu.VMEM)
         dma = pltpu.SemaphoreType.DMA
+        out = pltpu.VMEM
         y, dx, dgate, dwg, dwu, dwd = pl.pallas_call(
             functools.partial(ring_kernel, n_z),
-            out_shape=(jax.ShapeDtypeStruct((tok, d_model), BF16), jax.ShapeDtypeStruct((tok, d_model), BF16),
-                       jax.ShapeDtypeStruct((tok, top_k), F32), jax.ShapeDtypeStruct(wg_loc.shape, F32),
-                       jax.ShapeDtypeStruct(wu_loc.shape, F32), jax.ShapeDtypeStruct(wd_loc.shape, F32)),
+            out_shape=(out((tok, d_model), BF16), out((tok, d_model), BF16), out((top_k, tok), F32),
+                       out(wg_loc.shape, F32), out(wu_loc.shape, F32), out(wd_loc.shape, F32)),
             in_specs=[hbm, hbm, vm, vm, hbm, hbm, hbm],
-            out_specs=(vm, vm, vm, hbm, hbm, hbm),
+            out_specs=(vm, vm, vm, vm, vm, vm),
             scratch_shapes=[
                 pltpu.VMEM((n, 2, tok, d_model), BF16),
                 pltpu.VMEM((n, 2, experts, half), F32),
                 pltpu.VMEM((SLOTS, 2, tok, d_model), F32),
                 pltpu.VMEM((SLOTS, 2, experts, half), F32),
                 pltpu.VMEM((2, tok, d_model), F32),
-                pltpu.VMEM((2, tok, d_model), F32),
                 pltpu.VMEM((2, experts, half), F32),
-                pltpu.VMEM((2, experts, half), F32),
+                pltpu.VMEM((2, half, d_model), F32),
+                pltpu.VMEM((experts, half), F32),
                 pltpu.VMEM(wg_loc.shape, BF16), pltpu.VMEM(wu_loc.shape, BF16), pltpu.VMEM(wd_loc.shape, BF16),
-                pltpu.VMEM(wg_loc.shape, F32), pltpu.VMEM(wu_loc.shape, F32), pltpu.VMEM(wd_loc.shape, F32),
                 dma((5,)),
                 dma((n, 2)), dma((n, 2)), dma((n, 2)), dma((n, 2)), dma((n, 2)), dma((n, 2)),
-                dma((n, 2)), dma((n, 2)), dma((n, 2)), dma((n, 2)),
+                dma((n, 2)), dma((n, 2)), dma((n, 2)), dma((n, 2)), dma((3,)),
                 pltpu.SemaphoreType.REGULAR((2,)),
             ],
-            compiler_params=pltpu.CompilerParams(collective_id=0, has_side_effects=True, vmem_limit_bytes=60 * 1024 * 1024),
-        )(x_loc, dy_loc, idx_loc, gate_loc, wg_loc, wu_loc, wd_loc)
-        return y, dx, dgate, dwg, dwu, dwd
+            compiler_params=pltpu.CompilerParams(collective_id=0, has_side_effects=True, vmem_limit_bytes=48 * 2**20),
+        )(x_loc, dy_loc, idx_loc.T, gate_loc.T, wg_loc, wu_loc, wd_loc)
+        return y, dx, dgate.T, dwg, dwu, dwd
 
     return jax.shard_map(device_layer, mesh=mesh, in_specs=(tok_spec, tok_spec, tok_spec, weight_spec, weight_spec, weight_spec, tok_spec), out_specs=(tok_spec, tok_spec, tok_spec, grad_spec, grad_spec, grad_spec), check_vma=False)

time: 294 us -> 266 us (0.905)
  Pallas kernels: 274 us -> 256 us
  local copies, waits for them, and re-layouts: 18.8 us -> 8.22 us
    pallas_call x1, Pallas kernels: 274 us -> 256 us  [device_layer(): pl.pallas_call(functools.partial(ring_kernel, n_z), out_shape=(out((tok,...]
    unnamed x11 -> x6, local copies, waits for them, and re-layouts: 17.2 us -> 8.22 us
where the time goes in v3:
time: 266 us; the launch traced here: 265 us
  Pallas kernels  256 us (96%)
  local copies, waits for them, and re-layouts  8.22 us (3%)
    pallas_call x1, Pallas kernels, device_layer(): pl.pallas_call(functools.partial(ring_kernel, n_z), out_shape=(out((tok,...  256 us
    unnamed x6, local copies, waits for them, and re-layouts  8.22 us

profile of v3, /device:TPU:0, one launch (start us, length us, event | category | flops | bytes accessed | tf_op | source)
XLA Modules:
  0.0 264.8 jit_solution(1120309718155728129)
XLA Ops:
  0.6 255.9 %shard_map.118 = (bf16[256,1024]{1,0:T(8,128)(2,1)S(1)}, bf16[256,1024]{1,0:T(8,128)(2,1)S(1)}, f32[8,256]{1,0:T(8,128)S(1)}, f32[2,1024,512]{2,1,0:T(8,128)S(1)...) custom-call(bf16[256,1024]{1,0:T(8,128)(2,1)} %x_ref.1, bf16[256,1024]{1,0:T(8,128)(2,1)} %dy_ref.1, ...), custom_call_target="tpu_custom_call" | custom-call | tf_op jit(solution)/shard_map/pallas_call | solution.py:274
  256.6 0.8 copy.19
  257.4 0.6 copy.21
  258.0 0.8 copy.20
  258.8 2.0 copy.22
  260.8 2.0 copy.23
  262.8 2.0 copy.24

commit v4 on v3

v4 whole, which is shorter than its diff:
```python
import functools

import jax
import jax.numpy as jnp
from jax import lax
from jax.experimental import pallas as pl
from jax.experimental.pallas import tpu as pltpu
from jax.sharding import PartitionSpec as P

MESH = pl.DeviceIdType.MESH
F32 = jnp.float32
BF16 = jnp.bfloat16
SLOTS = 3


def mm(p, q, cp, cq):
    return lax.dot_general(p, q, (((cp,), (cq,)), ((), ())), preferred_element_type=F32)


def ring_kernel(n_z, x_ref, dy_ref, idx_ref, gate_ref, wg_ref, wu_ref, wd_ref,
                y_ref, dx_ref, dgate_ref, awg, awu, awd,
                xd, gt, acc, part, pb, wg, wu, wd,
                load_sem, xd_send, xd_far, xd_recv, gt_send, gt_far, gt_recv, acc_send, acc_recv, pb_recv, credit):
    top_k, tok = idx_ref.shape
    half = tok // 2
    exp_local = wg_ref.shape[0]
    n_q = 2 * n_z
    n = 2 * n_q
    experts = exp_local * n
    z = lax.axis_index('ei')
    eo = lax.axis_index('eo')
    ycoord, core = eo // 2, eo % 2
    q = z + ycoord * (n_q - 1 - 2 * z)
    me = 2 * q + core
    first_expert = (z * 4 + eo) * exp_local

    def device_at(pos):
        pos = lax.rem(pos + 2 * n, n)
        chip, c = pos // 2, pos % 2
        col = chip // n_z
        return {'ei': chip + col * (n_q - 1 - 2 * chip), 'eo': col * 2 + c}

    right, left = device_at(me + 1), device_at(me - 1)
    to = (right, left)
    far = (device_at(me + 2), device_at(me - 2))
    back = (left, right)
    partner = {'ei': z, 'eo': eo + 1 - 2 * core}
    leaves = (core == 1, core == 0)

    loads = [pltpu.make_async_copy(src, dst, load_sem.at[i]) for i, (src, dst) in enumerate(
        ((x_ref, xd.at[0, 0]), (dy_ref, xd.at[0, 1]), (wg_ref, wg), (wu_ref, wu), (wd_ref, wd)))]
    for c in loads:
        c.start()

    barrier = pltpu.get_barrier_semaphore()
    for nb in (left, right) + far:
        pl.semaphore_signal(barrier, inc=1, device_id=nb, device_id_type=MESH)

    row = lax.broadcasted_iota(jnp.int32, (experts, tok), 0)
    dense = jnp.zeros((experts, tok), F32)
    for j in range(top_k):
        dense = dense + jnp.where(row == idx_ref[j:j + 1, :], gate_ref[j:j + 1, :], 0.0)
    for d in range(2):
        gt[0, d] = dense[:, d * half:(d + 1) * half]
        part[d, tok:tok + 8] = jnp.zeros((8, part.shape[2]), F32)
    for e in range(exp_local):
        awg[e] = jnp.zeros(awg.shape[1:], F32)
        awu[e] = jnp.zeros(awu.shape[1:], F32)
        awd[e] = jnp.zeros(awd.shape[1:], F32)

    pl.semaphore_wait(barrier, 4)
    loads[0].wait()
    loads[1].wait()

    def rows(d):
        return pl.ds(d * half, half)

    def xd_copy(s, d):
        return pltpu.make_async_remote_copy(
            src_ref=xd.at[s, :, rows(d)], dst_ref=xd.at[s + 1, :, rows(d)], send_sem=xd_send.at[s, d],
            recv_sem=xd_recv.at[s, d], device_id=to[d], device_id_type=MESH)

    def gt_copy(s, d):
        return pltpu.make_async_remote_copy(
            src_ref=gt.at[s, d], dst_ref=gt.at[s + 1, d], send_sem=gt_send.at[s, d],
            recv_sem=gt_recv.at[s, d], device_id=to[d], device_id_type=MESH)

    def xd_skip(s, d):
        return pltpu.make_async_remote_copy(
            src_ref=xd.at[s, :, rows(d)], dst_ref=xd.at[s + 2, :, rows(d)], send_sem=xd_far.at[s, d],
            recv_sem=xd_recv.at[s + 1, d], device_id=far[d], device_id_type=MESH)

    def gt_skip(s, d):
        return pltpu.make_async_remote_copy(
            src_ref=gt.at[s, d], dst_ref=gt.at[s + 2, d], send_sem=gt_far.at[s, d],
            recv_sem=gt_recv.at[s + 1, d], device_id=far[d], device_id_type=MESH)

    def acc_copy(s, d):
        return pltpu.make_async_remote_copy(
            src_ref=acc.at[lax.rem(s, SLOTS), d], dst_ref=acc.at[lax.rem(s + 1, SLOTS), d],
            send_sem=acc_send.at[s, d], recv_sem=acc_recv.at[s, d], device_id=to[d], device_id_type=MESH)

    def xd_direct(d):
        return pltpu.make_async_remote_copy(
            src_ref=xd.at[0, :, rows(d)], dst_ref=xd.at[n - 1, :, rows(d)], send_sem=xd_send.at[n - 2, d],
            recv_sem=xd_recv.at[n - 2, d], device_id=partner, device_id_type=MESH)

    def gt_direct(d):
        return pltpu.make_async_remote_copy(
            src_ref=gt.at[0, d], dst_ref=gt.at[n - 1, d], send_sem=gt_send.at[n - 2, d],
            recv_sem=gt_recv.at[n - 2, d], device_id=partner, device_id_type=MESH)

    def pb_copy(d):
        return pltpu.make_async_remote_copy(
            src_ref=acc.at[1, d], dst_ref=pb, send_sem=acc_send.at[1, d],
            recv_sem=pb_recv.at[0], device_id=partner, device_id_type=MESH)

    def add_part(e, at, val):
        for d in range(2):
            here = pl.ds(at, half)
            part[d, here] = jnp.where(e == 0, 0.0, part[d, here]) + val[d * half:(d + 1) * half]

    def compute(s):
        wide = [jnp.concatenate([gt[s, d], jnp.zeros((128 - experts, half), F32)], axis=0).T for d in range(2)]
        gates = jnp.concatenate(wide, axis=0)

        def one(e, carry):
            dgs = carry
            lane_t = lax.broadcasted_iota(jnp.int32, (tok, 128), 1)
            mine = lane_t == first_expert + e
            gcol = jnp.sum(jnp.where(mine, gates, 0.0), axis=1, keepdims=True)
            routed = gcol > 0.0
            x = xd[s, 0]
            a = mm(x, wg[e], 1, 0)
            b = mm(x, wu[e], 1, 0)
            sig = jax.nn.sigmoid(a)
            silu = a * sig
            h = jnp.where(routed, silu * b, 0.0).astype(BF16)
            o = mm(h, wd[e], 1, 0).astype(BF16).astype(F32)
            dyf = xd[s, 1].astype(F32)
            add_part(e, 0, gcol * o)
            dg = jnp.sum(dyf * o, axis=1, keepdims=True)
            dgs = dgs + jnp.where(mine, dg, 0.0)
            g = (gcol * dyf).astype(BF16)
            awd[e] = awd[e] + mm(h, g, 0, 0)
            dh = mm(g, wd[e], 1, 1)
            da = jnp.where(routed, dh * b * sig * (1.0 + a * (1.0 - sig)), 0.0).astype(BF16)
            db = jnp.where(routed, dh * silu, 0.0).astype(BF16)
            awg[e] = awg[e] + mm(x, da, 0, 0)
            awu[e] = awu[e] + mm(x, db, 0, 0)
            dxr = (mm(da, wg[e], 1, 1) + mm(db, wu[e], 1, 1)).astype(BF16).astype(F32)
            add_part(e, half, dxr)
            return dgs

        dgs = lax.fori_loop(0, exp_local, one, jnp.zeros((tok, 128), F32))
        for d in range(2):
            dgt = dgs[d * half:(d + 1) * half].T
            for i in range(experts // 8):
                part[d, tok:tok + 8, i * 128:(i + 1) * 128] = dgt[8 * i:8 * i + 8]

    for d in range(2):
        gt_copy(0, d).start()
        xd_copy(0, d).start()
    for d in range(2):
        @pl.when(leaves[d])
        def _(d=d):
            gt_direct(d).start()
            xd_direct(d).start()

        @pl.when(jnp.logical_not(leaves[d]))
        def _(d=d):
            gt_skip(0, d).start()
            xd_skip(0, d).start()

    for c in loads[2:]:
        c.wait()

    def step(s, carry):
        slot = lax.rem(s, SLOTS)
        for d in range(2):
            gt_copy(s - 1, d).wait_recv()
            xd_copy(s - 1, d).wait_recv()

            @pl.when(jnp.logical_and(s <= n - 2, jnp.logical_not(leaves[d])))
            def _(d=d):
                gt_copy(s, d).start()
                xd_copy(s, d).start()

            @pl.when(jnp.logical_and(s <= n - 4, jnp.logical_not(leaves[d])))
            def _(d=d):
                gt_skip(s, d).start()
                xd_skip(s, d).start()

        compute(s)

        @pl.when(s >= 2)
        def _():
            for d in range(2):
                acc_copy(s - 1, d).wait_send()

        @pl.when(jnp.logical_and(s >= 2, s - 1 + SLOTS <= n))
        def _():
            for d in range(2):
                pl.semaphore_signal(credit.at[d], inc=1, device_id=back[d], device_id_type=MESH)

        @pl.when(s >= SLOTS)
        def _():
            for d in range(2):
                pl.semaphore_wait(credit.at[d], 1)

        for d in range(2):
            fresh = jnp.logical_or(s == 1, jnp.logical_and(s == 2, jnp.logical_not(leaves[d])))

            @pl.when(fresh)
            def _(d=d):
                acc[slot, d] = part[d]

            @pl.when(jnp.logical_not(fresh))
            def _(d=d):
                acc_copy(s - 1, d).wait_recv()
                acc[slot, d] = acc[slot, d] + part[d]

            @pl.when(jnp.logical_and(s == 1, leaves[d]))
            def _(d=d):
                pb_copy(d).start()

            @pl.when(jnp.logical_not(jnp.logical_and(s == 1, leaves[d])))
            def _(d=d):
                acc_copy(s, d).start()

        return carry

    lax.fori_loop(1, n, step, 0)

    compute(0)

    def drain(s, carry):
        for d in range(2):
            @pl.when(jnp.logical_or(jnp.logical_or(s == 0, s == n - 2), jnp.logical_not(leaves[d])))
            def _(d=d):
                gt_copy(s, d).wait_send()
                xd_copy(s, d).wait_send()

            @pl.when(jnp.logical_and(s <= n - 4, jnp.logical_not(leaves[d])))
            def _(d=d):
                gt_skip(s, d).wait_send()
                xd_skip(s, d).wait_send()

        return carry

    lax.fori_loop(0, n - 1, drain, 0)
    last = n % SLOTS
    for d in range(2):
        acc_copy(n - 1, d).wait_send()
    pb_copy(0).wait_recv()
    dgs = []
    for d in range(2):
        acc_copy(n - 1, d).wait_recv()
        for k, out in enumerate((y_ref, dx_ref)):
            here = pl.ds(k * half, half)
            out[rows(d)] = (acc[last, d, here] + part[d, here] + jnp.where(leaves[d], 0.0, pb[here])).astype(BF16)
        tail = acc[last, d, tok:tok + 8] + part[d, tok:tok + 8] + jnp.where(leaves[d], 0.0, pb[tok:tok + 8])
        dgs.append(jnp.concatenate([tail[:, i * 128:(i + 1) * 128] for i in range(experts // 8)], axis=0))
    dg_all = jnp.concatenate(dgs, axis=1)
    for j in range(top_k):
        dgate_ref[j:j + 1, :] = jnp.sum(jnp.where(row == idx_ref[j:j + 1, :], dg_all, 0.0), axis=0, keepdims=True)


def store_kernel(*refs):
    count = len(refs) // 2
    sems = refs[-1]
    copies = [pltpu.make_async_copy(refs[i], refs[count + i], sems.at[i]) for i in range(count)]
    for c in copies:
        c.start()
    for c in copies:
        c.wait()


def solution(mesh):
    n_z = mesh.shape['ei']
    n = n_z * mesh.shape['eo']
    tok_spec = P(('dp', 'ei', 'eo'), None)
    weight_spec = P(('ei', 'eo'), None, None)
    grad_spec = P(('dp', 'ei', 'eo'), None, None)

    def device_layer(x_loc, idx_loc, gate_loc, wg_loc, wu_loc, wd_loc, dy_loc):
        tok, top_k = idx_loc.shape
        d_model = x_loc.shape[1]
        exp_local, _, ff = wg_loc.shape
        experts = exp_local * n
        half = tok // 2
        hbm = pl.BlockSpec(memory_space=pl.ANY)
        vm = pl.BlockSpec(memory_space=pltpu.VMEM)
        dma = pltpu.SemaphoreType.DMA
        out = pltpu.VMEM
        results = pl.pallas_call(
            functools.partial(ring_kernel, n_z),
            out_shape=(out((tok, d_model), BF16), out((tok, d_model), BF16), out((top_k, tok), F32),
                       out(wg_loc.shape, F32), out(wu_loc.shape, F32), out(wd_loc.shape, F32)),
            in_specs=[hbm, hbm, vm, vm, hbm, hbm, hbm],
            out_specs=(vm, vm, vm, vm, vm, vm),
            scratch_shapes=[
                pltpu.VMEM((n, 2, tok, d_model), BF16),
                pltpu.VMEM((n, 2, experts, half), F32),
                pltpu.VMEM((SLOTS, 2, tok + 8, d_model), F32),
                pltpu.VMEM((2, tok + 8, d_model), F32),
                pltpu.VMEM((tok + 8, d_model), F32),
                pltpu.VMEM(wg_loc.shape, BF16), pltpu.VMEM(wu_loc.shape, BF16), pltpu.VMEM(wd_loc.shape, BF16),
                dma((5,)),
                dma((n, 2)), dma((n, 2)), dma((n, 2)), dma((n, 2)), dma((n, 2)), dma((n, 2)), dma((n, 2)), dma((n, 2)), dma((1,)),
                pltpu.SemaphoreType.REGULAR((2,)),
            ],
            compiler_params=pltpu.CompilerParams(collective_id=0, has_side_effects=True, vmem_limit_bytes=48 * 2**20),
        )(x_loc, dy_loc, idx_loc.T, gate_loc.T, wg_loc, wu_loc, wd_loc)
        y, dx, dgate, dwg, dwu, dwd = pl.pallas_call(
            store_kernel,
            out_shape=tuple(jax.ShapeDtypeStruct(r.shape, r.dtype) for r in results),
            in_specs=[vm] * len(results),
            out_specs=(hbm,) * len(results),
            scratch_shapes=[dma((len(results),))],
            compiler_params=pltpu.CompilerParams(vmem_limit_bytes=2**20),
        )(*[pltpu.with_memory_space_constraint(r, pltpu.VMEM) for r in results])
        return y, dx, dgate.T, dwg, dwu, dwd

    return jax.shard_map(device_layer, mesh=mesh, in_specs=(tok_spec, tok_spec, tok_spec, weight_spec, weight_spec, weight_spec, tok_spec), out_specs=(tok_spec, tok_spec, tok_spec, grad_spec, grad_spec, grad_spec), check_vma=False)
```

time: 266 us -> 278 us (1.045)
  Pallas kernels: 256 us -> 277 us
  local copies, waits for them, and re-layouts: 8.22 us -> 0 us
    pallas_call x1, Pallas kernels: 256 us -> 272 us  [device_layer(): pl.pallas_call(functools.partial(ring_kernel, n_z), out_shape=(out((tok,...]
    unnamed x6 -> x0, local copies, waits for them, and re-layouts: 8.22 us -> none
    pallas_call x0 -> x1, Pallas kernels: none -> 5.06 us  [device_layer(): pl.pallas_call(store_kernel, out_shape=tuple((jax.ShapeDtypeStruct(r.shap...]
where the time goes in v4:
time: 278 us; the launch traced here: 277 us
  Pallas kernels  277 us (100%)
    pallas_call x1, Pallas kernels, device_layer(): pl.pallas_call(functools.partial(ring_kernel, n_z), out_shape=(out((tok,...  272 us

profile of v4, /device:TPU:0, one launch (start us, length us, event | category | flops | bytes accessed | tf_op | source)
XLA Modules:
  0.0 277.4 jit_solution(15561935940003967824)
XLA Ops:
  0.6 271.7 %shard_map.118 = (bf16[256,1024]{1,0:T(8,128)(2,1)S(1)}, bf16[256,1024]{1,0:T(8,128)(2,1)S(1)}, f32[8,256]{1,0:T(8,128)S(1)}, f32[2,1024,512]{2,1,0:T(8,128)S(1)...) custom-call(bf16[256,1024]{1,0:T(8,128)(2,1)} %x_ref.1, bf16[256,1024]{1,0:T(8,128)(2,1)} %dy_ref.1, ...), custom_call_target="tpu_custom_call" | custom-call | tf_op jit(solution)/shard_map/pallas_call | solution.py:296
  272.3 5.1 %shard_map.119 = (bf16[256,1024]{1,0:T(8,128)(2,1)}, bf16[256,1024]{1,0:T(8,128)(2,1)}, f32[8,256]{1,0:T(8,128)}, f32[2,1024,512]{2,1,0:T(8,128)}, f32[2,1024,512]{2,1,0:T(8,128)}, /*index=5*/f32[2,512,1024]{2,1,0:T(8,128)}) custom-call(bf16[256,1024]{1,0:T(8,128)(2,1)S(1)} %get-tuple-element.18.refs_0_, bf16[256,1024]{1,0:T(8,128)(2,1)S(1)} %get-tuple-element.19.refs_1_, ...), custom_call_target="tpu_custom_call" | custom-call | tf_op jit(solution)/shard_map/pallas_call | solution.py:315

commit v5 on v4

--- a/solution.py
+++ b/solution.py
@@ -10,7 +10,7 @@
 MESH = pl.DeviceIdType.MESH
 F32 = jnp.float32
 BF16 = jnp.bfloat16
-SLOTS = 3
+SLOTS = 4
 
 
 def mm(p, q, cp, cq):
@@ -193,40 +193,43 @@
 
         compute(s)
 
-        @pl.when(s >= 2)
-        def _():
-            for d in range(2):
-                acc_copy(s - 1, d).wait_send()
-
-        @pl.when(jnp.logical_and(s >= 2, s - 1 + SLOTS <= n))
-        def _():
-            for d in range(2):
-                pl.semaphore_signal(credit.at[d], inc=1, device_id=back[d], device_id_type=MESH)
-
-        @pl.when(s >= SLOTS)
-        def _():
-            for d in range(2):
+        def pass_on(d):
+            fresh = jnp.logical_or(s == 1, jnp.logical_and(s == 2, jnp.logical_not(leaves[d])))
+
+            @pl.when(s >= SLOTS)
+            def _():
                 pl.semaphore_wait(credit.at[d], 1)
 
-        for d in range(2):
-            fresh = jnp.logical_or(s == 1, jnp.logical_and(s == 2, jnp.logical_not(leaves[d])))
-
             @pl.when(fresh)
-            def _(d=d):
+            def _():
                 acc[slot, d] = part[d]
 
             @pl.when(jnp.logical_not(fresh))
-            def _(d=d):
+            def _():
                 acc_copy(s - 1, d).wait_recv()
                 acc[slot, d] = acc[slot, d] + part[d]
 
             @pl.when(jnp.logical_and(s == 1, leaves[d]))
-            def _(d=d):
+            def _():
                 pb_copy(d).start()
 
             @pl.when(jnp.logical_not(jnp.logical_and(s == 1, leaves[d])))
-            def _(d=d):
+            def _():
                 acc_copy(s, d).start()
+
+        for d, first in ((0, True), (1, True), (0, False), (1, False)):
+            @pl.when(leaves[d] if first else jnp.logical_not(leaves[d]))
+            def _(d=d):
+                pass_on(d)
+
+        for d in range(2):
+            @pl.when(s >= 2)
+            def _(d=d):
+                acc_copy(s - 1, d).wait_send()
+
+            @pl.when(jnp.logical_and(s >= 2, s - 1 + SLOTS <= n))
+            def _(d=d):
+                pl.semaphore_signal(credit.at[d], inc=1, device_id=back[d], device_id_type=MESH)
 
         return carry
 

time: 278 us -> 261 us (0.939)
  Pallas kernels: 277 us -> 260 us
    pallas_call x1, Pallas kernels: 272 us -> 255 us  [device_layer(): pl.pallas_call(functools.partial(ring_kernel, n_z), out_shape=(out((tok,...]
where the time goes in v5:
time: 261 us
  Pallas kernels  260 us (100%)
    pallas_call x1, Pallas kernels, device_layer(): pl.pallas_call(functools.partial(ring_kernel, n_z), out_shape=(out((tok,...  255 us

profile of v5, /device:TPU:0, one launch (start us, length us, event | category | flops | bytes accessed | tf_op | source)
XLA Modules:
  0.0 260.8 jit_solution(1347795066954662737)
XLA Ops:
  0.6 255.1 %shard_map.118 = (bf16[256,1024]{1,0:T(8,128)(2,1)S(1)}, bf16[256,1024]{1,0:T(8,128)(2,1)S(1)}, f32[8,256]{1,0:T(8,128)S(1)}, f32[2,1024,512]{2,1,0:T(8,128)S(1)...) custom-call(bf16[256,1024]{1,0:T(8,128)(2,1)} %x_ref.1, bf16[256,1024]{1,0:T(8,128)(2,1)} %dy_ref.1, ...), custom_call_target="tpu_custom_call" | custom-call | tf_op jit(solution)/shard_map/pallas_call | solution.py:299
  255.8 5.1 %shard_map.119 = (bf16[256,1024]{1,0:T(8,128)(2,1)}, bf16[256,1024]{1,0:T(8,128)(2,1)}, f32[8,256]{1,0:T(8,128)}, f32[2,1024,512]{2,1,0:T(8,128)}, f32[2,1024,512]{2,1,0:T(8,128)}, /*index=5*/f32[2,512,1024]{2,1,0:T(8,128)}) custom-call(bf16[256,1024]{1,0:T(8,128)(2,1)S(1)} %get-tuple-element.18.refs_0_, bf16[256,1024]{1,0:T(8,128)(2,1)S(1)} %get-tuple-element.19.refs_1_, ...), custom_call_target="tpu_custom_call" | custom-call | tf_op jit(solution)/shard_map/pallas_call | solution.py:318

commit v6 on v5

--- a/solution.py
+++ b/solution.py
@@ -19,14 +19,14 @@
 
 def ring_kernel(n_z, x_ref, dy_ref, idx_ref, gate_ref, wg_ref, wu_ref, wd_ref,
                 y_ref, dx_ref, dgate_ref, awg, awu, awd,
-                xd, gt, acc, part, pb, wg, wu, wd,
-                load_sem, xd_send, xd_far, xd_recv, gt_send, gt_far, gt_recv, acc_send, acc_recv, pb_recv, credit):
+                xd, gt, acc, dga, part, dgp, pb, dgb, wg, wu, wd,
+                load_sem, xd_send, xd_far, xd_recv, gt_send, gt_far, gt_recv, acc_send, acc_recv, dg_send, dg_recv, pb_recv,
+                credit):
     top_k, tok = idx_ref.shape
     half = tok // 2
     exp_local = wg_ref.shape[0]
     n_q = 2 * n_z
     n = 2 * n_q
-    experts = exp_local * n
     z = lax.axis_index('ei')
     eo = lax.axis_index('eo')
     ycoord, core = eo // 2, eo % 2
@@ -56,13 +56,9 @@
     for nb in (left, right) + far:
         pl.semaphore_signal(barrier, inc=1, device_id=nb, device_id_type=MESH)
 
-    row = lax.broadcasted_iota(jnp.int32, (experts, tok), 0)
-    dense = jnp.zeros((experts, tok), F32)
-    for j in range(top_k):
-        dense = dense + jnp.where(row == idx_ref[j:j + 1, :], gate_ref[j:j + 1, :], 0.0)
-    for d in range(2):
-        gt[0, d] = dense[:, d * half:(d + 1) * half]
-        part[d, tok:tok + 8] = jnp.zeros((8, part.shape[2]), F32)
+    for d in range(2):
+        gt[0, d, :top_k] = idx_ref[:, d * half:(d + 1) * half].astype(F32)
+        gt[0, d, top_k:] = gate_ref[:, d * half:(d + 1) * half]
     for e in range(exp_local):
         awg[e] = jnp.zeros(awg.shape[1:], F32)
         awu[e] = jnp.zeros(awu.shape[1:], F32)
@@ -100,6 +96,11 @@
             src_ref=acc.at[lax.rem(s, SLOTS), d], dst_ref=acc.at[lax.rem(s + 1, SLOTS), d],
             send_sem=acc_send.at[s, d], recv_sem=acc_recv.at[s, d], device_id=to[d], device_id_type=MESH)
 
+    def dg_copy(s, d):
+        return pltpu.make_async_remote_copy(
+            src_ref=dga.at[lax.rem(s, SLOTS), d], dst_ref=dga.at[lax.rem(s + 1, SLOTS), d],
+            send_sem=dg_send.at[s, d], recv_sem=dg_recv.at[s, d], device_id=to[d], device_id_type=MESH)
+
     def xd_direct(d):
         return pltpu.make_async_remote_copy(
             src_ref=xd.at[0, :, rows(d)], dst_ref=xd.at[n - 1, :, rows(d)], send_sem=xd_send.at[n - 2, d],
@@ -115,19 +116,27 @@
             src_ref=acc.at[1, d], dst_ref=pb, send_sem=acc_send.at[1, d],
             recv_sem=pb_recv.at[0], device_id=partner, device_id_type=MESH)
 
+    def dgb_copy(d):
+        return pltpu.make_async_remote_copy(
+            src_ref=dga.at[1, d], dst_ref=dgb, send_sem=dg_send.at[1, d],
+            recv_sem=pb_recv.at[1], device_id=partner, device_id_type=MESH)
+
     def add_part(e, at, val):
         for d in range(2):
             here = pl.ds(at, half)
             part[d, here] = jnp.where(e == 0, 0.0, part[d, here]) + val[d * half:(d + 1) * half]
 
     def compute(s):
-        wide = [jnp.concatenate([gt[s, d], jnp.zeros((128 - experts, half), F32)], axis=0).T for d in range(2)]
-        gates = jnp.concatenate(wide, axis=0)
+        def columns(first, fill):
+            pad = jnp.full((128 - top_k, half), fill, F32)
+            return jnp.concatenate(
+                [jnp.concatenate([gt[s, d, first:first + top_k], pad], axis=0).T for d in range(2)], axis=0)
+
+        ids, gates = columns(0, -1.0), columns(top_k, 0.0)
 
         def one(e, carry):
             dgs = carry
-            lane_t = lax.broadcasted_iota(jnp.int32, (tok, 128), 1)
-            mine = lane_t == first_expert + e
+            mine = ids == (first_expert + e).astype(F32)
             gcol = jnp.sum(jnp.where(mine, gates, 0.0), axis=1, keepdims=True)
             routed = gcol > 0.0
             x = xd[s, 0]
@@ -154,9 +163,7 @@
 
         dgs = lax.fori_loop(0, exp_local, one, jnp.zeros((tok, 128), F32))
         for d in range(2):
-            dgt = dgs[d * half:(d + 1) * half].T
-            for i in range(experts // 8):
-                part[d, tok:tok + 8, i * 128:(i + 1) * 128] = dgt[8 * i:8 * i + 8]
+            dgp[d] = dgs[d * half:(d + 1) * half].T[:top_k]
 
     for d in range(2):
         gt_copy(0, d).start()
@@ -167,11 +174,6 @@
             gt_direct(d).start()
             xd_direct(d).start()
 
-        @pl.when(jnp.logical_not(leaves[d]))
-        def _(d=d):
-            gt_skip(0, d).start()
-            xd_skip(0, d).start()
-
     for c in loads[2:]:
         c.wait()
 
@@ -186,6 +188,11 @@
                 gt_copy(s, d).start()
                 xd_copy(s, d).start()
 
+            @pl.when(jnp.logical_and(s == 1, jnp.logical_not(leaves[d])))
+            def _(d=d):
+                gt_skip(0, d).start()
+                xd_skip(0, d).start()
+
             @pl.when(jnp.logical_and(s <= n - 4, jnp.logical_not(leaves[d])))
             def _(d=d):
                 gt_skip(s, d).start()
@@ -203,19 +210,24 @@
             @pl.when(fresh)
             def _():
                 acc[slot, d] = part[d]
+                dga[slot, d] = dgp[d]
 
             @pl.when(jnp.logical_not(fresh))
             def _():
                 acc_copy(s - 1, d).wait_recv()
                 acc[slot, d] = acc[slot, d] + part[d]
+                dg_copy(s - 1, d).wait_recv()
+                dga[slot, d] = dga[slot, d] + dgp[d]
 
             @pl.when(jnp.logical_and(s == 1, leaves[d]))
             def _():
                 pb_copy(d).start()
+                dgb_copy(d).start()
 
             @pl.when(jnp.logical_not(jnp.logical_and(s == 1, leaves[d])))
             def _():
                 acc_copy(s, d).start()
+                dg_copy(s, d).start()
 
         for d, first in ((0, True), (1, True), (0, False), (1, False)):
             @pl.when(leaves[d] if first else jnp.logical_not(leaves[d]))
@@ -226,6 +238,7 @@
             @pl.when(s >= 2)
             def _(d=d):
                 acc_copy(s - 1, d).wait_send()
+                dg_copy(s - 1, d).wait_send()
 
             @pl.when(jnp.logical_and(s >= 2, s - 1 + SLOTS <= n))
             def _(d=d):
@@ -255,18 +268,16 @@
     last = n % SLOTS
     for d in range(2):
         acc_copy(n - 1, d).wait_send()
+        dg_copy(n - 1, d).wait_send()
     pb_copy(0).wait_recv()
-    dgs = []
-    for d in range(2):
+    dgb_copy(0).wait_recv()
+    for d in range(2):
+        dg_copy(n - 1, d).wait_recv()
+        dgate_ref[:, d * half:(d + 1) * half] = dga[last, d] + dgp[d] + jnp.where(leaves[d], 0.0, dgb[...])
         acc_copy(n - 1, d).wait_recv()
         for k, out in enumerate((y_ref, dx_ref)):
             here = pl.ds(k * half, half)
             out[rows(d)] = (acc[last, d, here] + part[d, here] + jnp.where(leaves[d], 0.0, pb[here])).astype(BF16)
-        tail = acc[last, d, tok:tok + 8] + part[d, tok:tok + 8] + jnp.where(leaves[d], 0.0, pb[tok:tok + 8])
-        dgs.append(jnp.concatenate([tail[:, i * 128:(i + 1) * 128] for i in range(experts // 8)], axis=0))
-    dg_all = jnp.concatenate(dgs, axis=1)
-    for j in range(top_k):
-        dgate_ref[j:j + 1, :] = jnp.sum(jnp.where(row == idx_ref[j:j + 1, :], dg_all, 0.0), axis=0, keepdims=True)
 
 
 def store_kernel(*refs):
@@ -290,7 +301,6 @@
         tok, top_k = idx_loc.shape
         d_model = x_loc.shape[1]
         exp_local, _, ff = wg_loc.shape
-        experts = exp_local * n
         half = tok // 2
         hbm = pl.BlockSpec(memory_space=pl.ANY)
         vm = pl.BlockSpec(memory_space=pltpu.VMEM)
@@ -304,13 +314,17 @@
             out_specs=(vm, vm, vm, vm, vm, vm),
             scratch_shapes=[
                 pltpu.VMEM((n, 2, tok, d_model), BF16),
-                pltpu.VMEM((n, 2, experts, half), F32),
-                pltpu.VMEM((SLOTS, 2, tok + 8, d_model), F32),
-                pltpu.VMEM((2, tok + 8, d_model), F32),
-                pltpu.VMEM((tok + 8, d_model), F32),
+                pltpu.VMEM((n, 2, 2 * top_k, half), F32),
+                pltpu.VMEM((SLOTS, 2, tok, d_model), F32),
+                pltpu.VMEM((SLOTS, 2, top_k, half), F32),
+                pltpu.VMEM((2, tok, d_model), F32),
+                pltpu.VMEM((2, top_k, half), F32),
+                pltpu.VMEM((tok, d_model), F32),
+                pltpu.VMEM((top_k, half), F32),
                 pltpu.VMEM(wg_loc.shape, BF16), pltpu.VMEM(wu_loc.shape, BF16), pltpu.VMEM(wd_loc.shape, BF16),
                 dma((5,)),
-                dma((n, 2)), dma((n, 2)), dma((n, 2)), dma((n, 2)), dma((n, 2)), dma((n, 2)), dma((n, 2)), dma((n, 2)), dma((1,)),
+                dma((n, 2)), dma((n, 2)), dma((n, 2)), dma((n, 2)), dma((n, 2)), dma((n, 2)), dma((n, 2)), dma((n, 2)),
+                dma((n, 2)), dma((n, 2)), dma((2,)),
                 pltpu.SemaphoreType.REGULAR((2,)),
             ],
             compiler_params=pltpu.CompilerParams(collective_id=0, has_side_effects=True, vmem_limit_bytes=48 * 2**20),

time: 261 us -> 256 us (0.981)
  Pallas kernels: 260 us -> 255 us
    pallas_call x1, Pallas kernels: 255 us -> 250 us  [device_layer(): pl.pallas_call(functools.partial(ring_kernel, n_z), out_shape=(out((tok,...]
where the time goes in v6:
time: 256 us
  Pallas kernels  255 us (100%)
    pallas_call x1, Pallas kernels, device_layer(): pl.pallas_call(functools.partial(ring_kernel, n_z), out_shape=(out((tok,...  250 us

profile of v6, /device:TPU:0, one launch (start us, length us, event | category | flops | bytes accessed | tf_op | source)
XLA Modules:
  0.0 255.6 jit_solution(12322746086458246426)
XLA Ops:
  0.6 249.9 %shard_map.118 = (bf16[256,1024]{1,0:T(8,128)(2,1)S(1)}, bf16[256,1024]{1,0:T(8,128)(2,1)S(1)}, f32[8,256]{1,0:T(8,128)S(1)}, f32[2,1024,512]{2,1,0:T(8,128)S(1)...) custom-call(bf16[256,1024]{1,0:T(8,128)(2,1)} %x_ref.1, bf16[256,1024]{1,0:T(8,128)(2,1)} %dy_ref.1, ...), custom_call_target="tpu_custom_call" | custom-call | tf_op jit(solution)/shard_map/pallas_call | solution.py:309
  250.5 5.1 %shard_map.119 = (bf16[256,1024]{1,0:T(8,128)(2,1)}, bf16[256,1024]{1,0:T(8,128)(2,1)}, f32[8,256]{1,0:T(8,128)}, f32[2,1024,512]{2,1,0:T(8,128)}, f32[2,1024,512]{2,1,0:T(8,128)}, /*index=5*/f32[2,512,1024]{2,1,0:T(8,128)}) custom-call(bf16[256,1024]{1,0:T(8,128)(2,1)S(1)} %get-tuple-element.18.refs_0_, bf16[256,1024]{1,0:T(8,128)(2,1)S(1)} %get-tuple-element.19.refs_1_, ...), custom_call_target="tpu_custom_call" | custom-call | tf_op jit(solution)/shard_map/pallas_call | solution.py:332

commit v7 on v6

--- a/solution.py
+++ b/solution.py
@@ -59,11 +59,6 @@
     for d in range(2):
         gt[0, d, :top_k] = idx_ref[:, d * half:(d + 1) * half].astype(F32)
         gt[0, d, top_k:] = gate_ref[:, d * half:(d + 1) * half]
-    for e in range(exp_local):
-        awg[e] = jnp.zeros(awg.shape[1:], F32)
-        awu[e] = jnp.zeros(awu.shape[1:], F32)
-        awd[e] = jnp.zeros(awd.shape[1:], F32)
-
     pl.semaphore_wait(barrier, 4)
     loads[0].wait()
     loads[1].wait()
@@ -174,6 +169,11 @@
             gt_direct(d).start()
             xd_direct(d).start()
 
+    for e in range(exp_local):
+        awg[e] = jnp.zeros(awg.shape[1:], F32)
+        awu[e] = jnp.zeros(awu.shape[1:], F32)
+        awd[e] = jnp.zeros(awd.shape[1:], F32)
+
     for c in loads[2:]:
         c.wait()
 
@@ -183,15 +183,10 @@
             gt_copy(s - 1, d).wait_recv()
             xd_copy(s - 1, d).wait_recv()
 
-            @pl.when(jnp.logical_and(s <= n - 2, jnp.logical_not(leaves[d])))
+            @pl.when(jnp.logical_and(s <= n - 2, jnp.logical_or(s == 1, jnp.logical_not(leaves[d]))))
             def _(d=d):
                 gt_copy(s, d).start()
                 xd_copy(s, d).start()
-
-            @pl.when(jnp.logical_and(s == 1, jnp.logical_not(leaves[d])))
-            def _(d=d):
-                gt_skip(0, d).start()
-                xd_skip(0, d).start()
 
             @pl.when(jnp.logical_and(s <= n - 4, jnp.logical_not(leaves[d])))
             def _(d=d):
@@ -252,12 +247,12 @@
 
     def drain(s, carry):
         for d in range(2):
-            @pl.when(jnp.logical_or(jnp.logical_or(s == 0, s == n - 2), jnp.logical_not(leaves[d])))
+            @pl.when(jnp.logical_or(jnp.logical_or(s <= 1, s == n - 2), jnp.logical_not(leaves[d])))
             def _(d=d):
                 gt_copy(s, d).wait_send()
                 xd_copy(s, d).wait_send()
 
-            @pl.when(jnp.logical_and(s <= n - 4, jnp.logical_not(leaves[d])))
+            @pl.when(jnp.logical_and(jnp.logical_and(s >= 1, s <= n - 4), jnp.logical_not(leaves[d])))
             def _(d=d):
                 gt_skip(s, d).wait_send()
                 xd_skip(s, d).wait_send()

time: 256 us -> 256 us (level)
  no operation moved by 1% of the time
where the time goes in v7:
time: 256 us; the launch traced here: 254 us
  Pallas kernels  254 us (99%)
    pallas_call x1, Pallas kernels, device_layer(): pl.pallas_call(functools.partial(ring_kernel, n_z), out_shape=(out((tok,...  249 us

profile of v7, /device:TPU:0, one launch (start us, length us, event | category | flops | bytes accessed | tf_op | source)
XLA Modules:
  0.0 254.4 jit_solution(14777762906362179487)
XLA Ops:
  0.6 248.7 %shard_map.118 = (bf16[256,1024]{1,0:T(8,128)(2,1)S(1)}, bf16[256,1024]{1,0:T(8,128)(2,1)S(1)}, f32[8,256]{1,0:T(8,128)S(1)}, f32[2,1024,512]{2,1,0:T(8,128)S(1)...) custom-call(bf16[256,1024]{1,0:T(8,128)(2,1)} %x_ref.1, bf16[256,1024]{1,0:T(8,128)(2,1)} %dy_ref.1, ...), custom_call_target="tpu_custom_call" | custom-call | tf_op jit(solution)/shard_map/pallas_call | solution.py:304
  249.4 5.1 %shard_map.119 = (bf16[256,1024]{1,0:T(8,128)(2,1)}, bf16[256,1024]{1,0:T(8,128)(2,1)}, f32[8,256]{1,0:T(8,128)}, f32[2,1024,512]{2,1,0:T(8,128)}, f32[2,1024,512]{2,1,0:T(8,128)}, /*index=5*/f32[2,512,1024]{2,1,0:T(8,128)}) custom-call(bf16[256,1024]{1,0:T(8,128)(2,1)S(1)} %get-tuple-element.18.refs_0_, bf16[256,1024]{1,0:T(8,128)(2,1)S(1)} %get-tuple-element.19.refs_1_, ...), custom_call_target="tpu_custom_call" | custom-call | tf_op jit(solution)/shard_map/pallas_call | solution.py:327

commit v8 on v7

--- a/solution.py
+++ b/solution.py
@@ -174,24 +174,40 @@
         awu[e] = jnp.zeros(awu.shape[1:], F32)
         awd[e] = jnp.zeros(awd.shape[1:], F32)
 
+    for d in range(2):
+        @pl.when(leaves[d])
+        def _(d=d):
+            gt_copy(0, d).wait_recv()
+            xd_copy(0, d).wait_recv()
+            gt_copy(1, d).start()
+            xd_copy(1, d).start()
+
     for c in loads[2:]:
         c.wait()
 
     def step(s, carry):
         slot = lax.rem(s, SLOTS)
         for d in range(2):
-            gt_copy(s - 1, d).wait_recv()
-            xd_copy(s - 1, d).wait_recv()
-
-            @pl.when(jnp.logical_and(s <= n - 2, jnp.logical_or(s == 1, jnp.logical_not(leaves[d]))))
-            def _(d=d):
-                gt_copy(s, d).start()
-                xd_copy(s, d).start()
-
-            @pl.when(jnp.logical_and(s <= n - 4, jnp.logical_not(leaves[d])))
-            def _(d=d):
-                gt_skip(s, d).start()
-                xd_skip(s, d).start()
+            @pl.when(jnp.logical_not(leaves[d]))
+            def _(d=d):
+                gt_copy(s - 1, d).wait_recv()
+                xd_copy(s - 1, d).wait_recv()
+
+                @pl.when(s <= n - 2)
+                def _():
+                    gt_copy(s, d).start()
+                    xd_copy(s, d).start()
+
+                @pl.when(s <= n - 4)
+                def _():
+                    gt_skip(s, d).start()
+                    xd_skip(s, d).start()
+
+        for d in range(2):
+            @pl.when(jnp.logical_and(s >= 2, leaves[d]))
+            def _(d=d):
+                gt_copy(s - 1, d).wait_recv()
+                xd_copy(s - 1, d).wait_recv()
 
         compute(s)
 

time: 256 us -> 254 us (level)
  no operation moved by 1% of the time
where the time goes in v8:
time: 254 us; the launch traced here: 253 us
  Pallas kernels  253 us (100%)
    pallas_call x1, Pallas kernels, device_layer(): pl.pallas_call(functools.partial(ring_kernel, n_z), out_shape=(out((tok,...  248 us

profile of v8, /device:TPU:0, one launch (start us, length us, event | category | flops | bytes accessed | tf_op | source)
XLA Modules:
  0.0 253.5 jit_solution(8982458289052328029)
XLA Ops:
  0.6 247.8 %shard_map.118 = (bf16[256,1024]{1,0:T(8,128)(2,1)S(1)}, bf16[256,1024]{1,0:T(8,128)(2,1)S(1)}, f32[8,256]{1,0:T(8,128)S(1)}, f32[2,1024,512]{2,1,0:T(8,128)S(1)...) custom-call(bf16[256,1024]{1,0:T(8,128)(2,1)} %x_ref.1, bf16[256,1024]{1,0:T(8,128)(2,1)} %dy_ref.1, ...), custom_call_target="tpu_custom_call" | custom-call | tf_op jit(solution)/shard_map/pallas_call | solution.py:320
  248.4 5.1 %shard_map.119 = (bf16[256,1024]{1,0:T(8,128)(2,1)}, bf16[256,1024]{1,0:T(8,128)(2,1)}, f32[8,256]{1,0:T(8,128)}, f32[2,1024,512]{2,1,0:T(8,128)}, f32[2,1024,512]{2,1,0:T(8,128)}, /*index=5*/f32[2,512,1024]{2,1,0:T(8,128)}) custom-call(bf16[256,1024]{1,0:T(8,128)(2,1)S(1)} %get-tuple-element.18.refs_0_, bf16[256,1024]{1,0:T(8,128)(2,1)S(1)} %get-tuple-element.19.refs_1_, ...), custom_call_target="tpu_custom_call" | custom-call | tf_op jit(solution)/shard_map/pallas_call | solution.py:343

commit v9 on v8

--- a/solution.py
+++ b/solution.py
@@ -277,18 +277,30 @@
 
     lax.fori_loop(0, n - 1, drain, 0)
     last = n % SLOTS
-    for d in range(2):
-        acc_copy(n - 1, d).wait_send()
-        dg_copy(n - 1, d).wait_send()
     pb_copy(0).wait_recv()
     dgb_copy(0).wait_recv()
-    for d in range(2):
+
+    def finish(d, extra, dg_extra):
         dg_copy(n - 1, d).wait_recv()
-        dgate_ref[:, d * half:(d + 1) * half] = dga[last, d] + dgp[d] + jnp.where(leaves[d], 0.0, dgb[...])
+        dgate_ref[:, d * half:(d + 1) * half] = dga[last, d] + dgp[d] + dg_extra
         acc_copy(n - 1, d).wait_recv()
         for k, out in enumerate((y_ref, dx_ref)):
             here = pl.ds(k * half, half)
-            out[rows(d)] = (acc[last, d, here] + part[d, here] + jnp.where(leaves[d], 0.0, pb[here])).astype(BF16)
+            out[rows(d)] = (acc[last, d, here] + part[d, here] + extra(here)).astype(BF16)
+
+    for d in range(2):
+        @pl.when(leaves[d])
+        def _(d=d):
+            finish(d, lambda here: 0.0, 0.0)
+
+    for d in range(2):
+        @pl.when(jnp.logical_not(leaves[d]))
+        def _(d=d):
+            finish(d, lambda here: pb[here], dgb[...])
+
+    for d in range(2):
+        acc_copy(n - 1, d).wait_send()
+        dg_copy(n - 1, d).wait_send()
 
 
 def store_kernel(*refs):

time: 254 us -> 254 us (level)
  no operation moved by 1% of the time
where the time goes in v9:
time: 254 us; the launch traced here: 253 us
  Pallas kernels  253 us (100%)
    pallas_call x1, Pallas kernels, device_layer(): pl.pallas_call(functools.partial(ring_kernel, n_z), out_shape=(out((tok,...  248 us

profile of v9, /device:TPU:0, one launch (start us, length us, event | category | flops | bytes accessed | tf_op | source)
XLA Modules:
  0.0 253.3 jit_solution(13970239590372918915)
XLA Ops:
  0.6 247.6 %shard_map.118 = (bf16[256,1024]{1,0:T(8,128)(2,1)S(1)}, bf16[256,1024]{1,0:T(8,128)(2,1)S(1)}, f32[8,256]{1,0:T(8,128)S(1)}, f32[2,1024,512]{2,1,0:T(8,128)S(1)...) custom-call(bf16[256,1024]{1,0:T(8,128)(2,1)} %x_ref.1, bf16[256,1024]{1,0:T(8,128)(2,1)} %dy_ref.1, ...), custom_call_target="tpu_custom_call" | custom-call | tf_op jit(solution)/shard_map/pallas_call | solution.py:332
  248.3 5.1 %shard_map.119 = (bf16[256,1024]{1,0:T(8,128)(2,1)}, bf16[256,1024]{1,0:T(8,128)(2,1)}, f32[8,256]{1,0:T(8,128)}, f32[2,1024,512]{2,1,0:T(8,128)}, f32[2,1024,512]{2,1,0:T(8,128)}, /*index=5*/f32[2,512,1024]{2,1,0:T(8,128)}) custom-call(bf16[256,1024]{1,0:T(8,128)(2,1)S(1)} %get-tuple-element.18.refs_0_, bf16[256,1024]{1,0:T(8,128)(2,1)S(1)} %get-tuple-element.19.refs_1_, ...), custom_call_target="tpu_custom_call" | custom-call | tf_op jit(solution)/shard_map/pallas_call | solution.py:355

commit v10 on v9

--- a/solution.py
+++ b/solution.py
@@ -306,7 +306,13 @@
 def store_kernel(*refs):
     count = len(refs) // 2
     sems = refs[-1]
-    copies = [pltpu.make_async_copy(refs[i], refs[count + i], sems.at[i]) for i in range(count)]
+    pairs = []
+    for src, dst in zip(refs[:count], refs[count:2 * count]):
+        if len(src.shape) == 3:
+            pairs += [(src.at[e], dst.at[e]) for e in range(src.shape[0])]
+        else:
+            pairs.append((src, dst))
+    copies = [pltpu.make_async_copy(src, dst, sems.at[i]) for i, (src, dst) in enumerate(pairs)]
     for c in copies:
         c.start()
     for c in copies:
@@ -357,7 +363,7 @@
             out_shape=tuple(jax.ShapeDtypeStruct(r.shape, r.dtype) for r in results),
             in_specs=[vm] * len(results),
             out_specs=(hbm,) * len(results),
-            scratch_shapes=[dma((len(results),))],
+            scratch_shapes=[dma((3 + 3 * exp_local,))],
             compiler_params=pltpu.CompilerParams(vmem_limit_bytes=2**20),
         )(*[pltpu.with_memory_space_constraint(r, pltpu.VMEM) for r in results])
         return y, dx, dgate.T, dwg, dwu, dwd

time: 254 us -> 254 us (level)
  no operation moved by 1% of the time
where the time goes in v10:
time: 254 us; the launch traced here: 253 us
  Pallas kernels  253 us (100%)
    pallas_call x1, Pallas kernels, device_layer(): pl.pallas_call(functools.partial(ring_kernel, n_z), out_shape=(out((tok,...  248 us

profile of v10, /device:TPU:0, one launch (start us, length us, event | category | flops | bytes accessed | tf_op | source)
XLA Modules:
  0.0 253.3 jit_solution(9117189127252254020)
XLA Ops:
  0.6 247.6 %shard_map.118 = (bf16[256,1024]{1,0:T(8,128)(2,1)S(1)}, bf16[256,1024]{1,0:T(8,128)(2,1)S(1)}, f32[8,256]{1,0:T(8,128)S(1)}, f32[2,1024,512]{2,1,0:T(8,128)S(1)...) custom-call(bf16[256,1024]{1,0:T(8,128)(2,1)} %x_ref.1, bf16[256,1024]{1,0:T(8,128)(2,1)} %dy_ref.1, ...), custom_call_target="tpu_custom_call" | custom-call | tf_op jit(solution)/shard_map/pallas_call | solution.py:338
  248.3 5.0 %shard_map.119 = (bf16[256,1024]{1,0:T(8,128)(2,1)}, bf16[256,1024]{1,0:T(8,128)(2,1)}, f32[8,256]{1,0:T(8,128)}, f32[2,1024,512]{2,1,0:T(8,128)}, f32[2,1024,512]{2,1,0:T(8,128)}, /*index=5*/f32[2,512,1024]{2,1,0:T(8,128)}) custom-call(bf16[256,1024]{1,0:T(8,128)(2,1)S(1)} %get-tuple-element.18.refs_0_, bf16[256,1024]{1,0:T(8,128)(2,1)S(1)} %get-tuple-element.19.refs_1_, ...), custom_call_target="tpu_custom_call" | custom-call | tf_op jit(solution)/shard_map/pallas_call | solution.py:361
